TPU v7x, 256 devices: a whole 4x4x8 slice. The times are simulated.
256 devices in a mesh: row: 32 (over z, y), feat: 8 (over x, core).
Axes of the slice: x: 4, y: 4, z: 8, core: 2. Of those that a mesh axis runs over, the one named last changes fastest.
Arguments:
- design: bfloat16 [4096, 65536], P('row', 'feat'), may hold values from -0.0234375 to 0.0234375
- targets: bfloat16 [4096, 48], P('row'), may hold values from -6 to 6
- factor: float32 [65536, 256], P(('feat', 'row')), may hold values from -0.09375 to 0.09375
- weights: float32 [256], replicated, may hold values from 0.3 to 3
- penalty: float32 [48], replicated, may hold values from 0.05 to 0.5
Outputs:
- solution: float32 [65536, 48], P(('feat', 'row'))
- residual: float32 [65536, 48], P(('feat', 'row'))
All inputs are finite; a program needn't handle non-finite values.
Results may differ from a plain program's by a relative error of at most 0.024.
Values may be sent and summed in bfloat16 or wider, within the bound.
No kernel may reach another device: no remote copies, remote signals or barrier semaphores. Data moves between devices by JAX's collectives and lax.ppermute only.
A program may use at most 64 MiB of HBM per device.

v0:
```python
import jax
import jax.numpy as jnp
from jax import lax
from jax.sharding import Mesh
from jax.sharding import PartitionSpec as P

ITERS = 3
ROW = ("row_0", "row_1")
ROW_FEAT = ("row_0", "row_1", "feat_0", "feat_1")
FEAT = ("feat_0", "feat_1")
FEAT_ROW = ("feat_0", "feat_1", "row_0", "row_1")


def in_blocks(shard, dim, devices):
    lengths = shard.shape
    pieces = shard.reshape(*lengths[:dim], devices, lengths[dim] // devices, *lengths[dim + 1 :])
    return jnp.moveaxis(pieces, dim, 0)


def summed_on_arrival(shard, axis, dim):
    pieces = in_blocks(shard, dim, lax.axis_size(axis))
    arrived = lax.all_to_all(pieces, axis, split_axis=0, concat_axis=0, tiled=True)
    return arrived.sum(axis=0)


def joined_along(pieces, dim):
    lengths = list(pieces.shape[1:])
    lengths[dim] *= pieces.shape[0]
    return jnp.moveaxis(pieces, 0, dim).reshape(lengths)


def copy_for_each(shard, axis):
    devices = lax.axis_size(axis)
    return lax.all_to_all(
        jnp.broadcast_to(shard[None], (devices, *shard.shape)), axis, 0, 0, tiled=True
    )


def collect(shard, axis, dim):
    return joined_along(copy_for_each(shard, axis), dim)


def one_axis_at_a_time(shard, axes):
    for axis in axes:
        shard = lax.psum(shard, axis)
    return shard


def taken_together(shard, axis):
    return copy_for_each(shard, axis).sum(axis=0)


def shards(design, targets, factor, weights, penalty):

    def normal_terms(rows_low):
        return summed_on_arrival(
            lax.dot_general(
                design, rows_low, (((0,), (0,)), ((), ())), preferred_element_type=jnp.float32
            ),
            ROW,
            0,
        )

    def precondition(residual):
        projected = jnp.dot(factor.T, residual, precision=lax.Precision.HIGHEST)
        projected, squares = (
            one_axis_at_a_time(projected, ROW_FEAT),
            one_axis_at_a_time(jnp.sum(residual * residual, axis=0), ROW_FEAT),
        )
        search = residual + jnp.dot(
            factor, weights[:, None] * projected, precision=lax.Precision.HIGHEST
        )
        inner = squares + jnp.sum(weights[:, None] * projected * projected, axis=0)
        return (search, inner)

    residual = normal_terms(targets)
    solution = jnp.zeros_like(residual)
    search, inner = precondition(residual)
    direction = search
    for step_index in range(ITERS):
        dir_low = direction.astype(jnp.bfloat16)
        row_values = taken_together(
            jnp.dot(design, collect(dir_low, ROW, 0), preferred_element_type=jnp.float32), FEAT
        )
        row_low = row_values.astype(jnp.bfloat16)
        dir_slice = direction
        local_part = jnp.sum(row_values * row_low.astype(jnp.float32), axis=0) / lax.axis_size(FEAT)
        local_part = local_part + penalty * jnp.sum(dir_slice * dir_slice, axis=0)
        curvature = one_axis_at_a_time(local_part, ROW_FEAT)
        hessian_dir = normal_terms(row_low) + penalty[None, :] * dir_slice
        step_size = inner / curvature
        solution = solution + step_size[None, :] * dir_slice
        residual = residual - step_size[None, :] * hessian_dir
        if step_index + 1 < ITERS:
            search, inner_next = precondition(residual)
            direction = search + (inner_next / inner)[None, :] * direction
            inner = inner_next
    return (solution, residual)


def solution(mesh):
    finer = Mesh(mesh.devices.reshape(8, 4, 4, 2), ("row_0", "row_1", "feat_0", "feat_1"))
    in_specs = (P(ROW, FEAT), P(ROW, None), P(FEAT_ROW, None), P(), P())
    out_specs = (P(FEAT_ROW, None), P(FEAT_ROW, None))
    return jax.shard_map(
        shards, mesh=finer, in_specs=in_specs, out_specs=out_specs, check_vma=False
    )
```

profile of v0, /device:TPU:1, one launch (start us, length us, event | category | flops | bytes accessed | tf_op | source)
XLA Modules:
  0.0 600.1 jit_solution(5762411116982464792)
XLA Ops:
  0.6 1.6 copy-done
  2.2 1.1 fusion.24
  3.6 50.7 %all_to_all.50 = f32[32,256,48]{1,2,0:T(8,128)} all-to-all(f32[32,256,48]{1,2,0:T(8,128)S(1)} %bitcast.76), channel_id=1, replica_groups=mesh['row_0'=8,'row_1'=4,'feat_0'=4,'feat_1'=2] {'row_0','row_1'}, dimensions={0} | all-to-all | bytes 3145728 | tf_op jit(solution)/shard_map/all_to_all | solution.py:22
  54.2 1.5 reduce_sum.171
  56.0 20.8 %psum.256 = f32[256,48]{0,1:T(8,128)S(1)} all-reduce(f32[256,48]{0,1:T(8,128)S(1)} %convolution_bitcast_fusion.5), channel_id=1, replica_groups=mesh['row_0'=8,'row_1'=4,'feat_0'=4,'feat_1'=2] {'row_0'}, use_global_device_ids=true, to_apply=%region_6.0 | all-reduce | flops 12288 | bytes 98304 | tf_op jit(solution)/shard_map/psum | solution.py:45
  76.9 13.6 %psum.257 = f32[256,48]{0,1:T(8,128)S(1)} all-reduce(f32[256,48]{0,1:T(8,128)S(1)} %psum.256), channel_id=1, replica_groups=mesh['row_0'=8,'row_1'=4,'feat_0'=4,'feat_1'=2] {'row_1'}, use_global_device_ids=true, to_apply=%region_7.0 | all-reduce | flops 12288 | bytes 98304 | tf_op jit(solution)/shard_map/psum | solution.py:45
  90.5 13.6 %psum.258 = f32[256,48]{0,1:T(8,128)S(1)} all-reduce(f32[256,48]{0,1:T(8,128)S(1)} %psum.257), channel_id=1, replica_groups=mesh['row_0'=8,'row_1'=4,'feat_0'=4,'feat_1'=2] {'feat_0'}, use_global_device_ids=true, to_apply=%region_8.0 | all-reduce | flops 12288 | bytes 98304 | tf_op jit(solution)/shard_map/psum | solution.py:45
  104.1 19.9 %psum.259 = f32[256,48]{0,1:T(8,128)S(1)} all-reduce(f32[256,48]{0,1:T(8,128)S(1)} %psum.258), channel_id=1, replica_groups=mesh['row_0'=8,'row_1'=4,'feat_0'=4,'feat_1'=2] {'feat_1'}, use_global_device_ids=true, to_apply=%region_9.0 | all-reduce | flops 12288 | bytes 98304 | tf_op jit(solution)/shard_map/psum | solution.py:45
  124.5 26.4 %all_to_all.51 = bf16[32,256,48]{1,2,0:T(8,128)(2,1)S(1)} all-to-all(bf16[32,256,48]{1,2,0:T(8,128)(2,1)S(1)} %broadcast_in_dim.12), channel_id=1, replica_groups=mesh['row_0'=8,'row_1'=4,'feat_0'=4,'feat_1'=2] {'row_0','row_1'}, dimensions={0} | all-to-all | bytes 1572864 | tf_op jit(solution)/shard_map/all_to_all | solution.py:34
  150.9 0.8 convolution_bitcast_fusion.8
  151.8 10.5 %all_to_all.52 = f32[8,128,48]{1,2,0:T(8,128)S(1)} all-to-all(f32[8,128,48]{1,2,0:T(8,128)S(1)} %broadcast_in_dim.13), channel_id=1, replica_groups=mesh['row_0'=8,'row_1'=4,'feat_0'=4,'feat_1'=2] {'feat_0','feat_1'}, dimensions={0} | all-to-all | bytes 393216 | tf_op jit(solution)/shard_map/all_to_all | solution.py:34
  162.7 1.4 copy.44
  164.1 5.2 all-to-all-start.3
  169.6 41.7 %all-reduce.2 = (f32[48]{0:T(128)S(1)}, f32[48]{0:T(128)S(1)}) all-reduce(f32[48]{0:T(128)S(1)} %multiply_reduce_fusion.5, f32[48]{0:T(128)S(1)} %multiply_add_fusion.3), channel_id=1, replica_groups=mesh['row_0'=8,'row_1'=4,'feat_0'=4,'feat_1'=2] {'row_0'}, use_global_device_ids=true, to_apply=%region_2.0 | all-reduce | flops 96 | bytes 768 | tf_op jit(solution)/shard_map/psum | solution.py:45
  211.3 9.2 %all-reduce.8 = (f32[48]{0:T(128)S(1)}, f32[48]{0:T(128)S(1)}) all-reduce(f32[48]{0:T(128)S(1)} %get-tuple-element.6, f32[48]{0:T(128)S(1)} %get-tuple-element.7), channel_id=1, replica_groups=mesh['row_0'=8,'row_1'=4,'feat_0'=4,'feat_1'=2] {'row_1'}, use_global_device_ids=true, to_apply=%region_3.0 | all-reduce | flops 96 | bytes 768 | tf_op jit(solution)/shard_map/psum | solution.py:45
  220.5 6.9 %all-reduce.5 = (f32[48]{0:T(128)S(1)}, f32[48]{0:T(128)S(1)}) all-reduce(f32[48]{0:T(128)S(1)} %get-tuple-element.18, f32[48]{0:T(128)S(1)} %get-tuple-element.19), channel_id=1, replica_groups=mesh['row_0'=8,'row_1'=4,'feat_0'=4,'feat_1'=2] {'feat_0'}, use_global_device_ids=true, to_apply=%region_4.0 | all-reduce | flops 96 | bytes 768 | tf_op jit(solution)/shard_map/psum | solution.py:45
  227.4 10.3 %all-reduce.11 = (f32[48]{0:T(128)S(1)}, f32[48]{0:T(128)S(1)}) all-reduce(f32[48]{0:T(128)S(1)} %get-tuple-element.12, f32[48]{0:T(128)S(1)} %get-tuple-element.13), channel_id=1, replica_groups=mesh['row_0'=8,'row_1'=4,'feat_0'=4,'feat_1'=2] {'feat_1'}, use_global_device_ids=true, to_apply=%region_5.0 | all-reduce | flops 96 | bytes 768 | tf_op jit(solution)/shard_map/psum | solution.py:45
  237.7 1.5 reduce_sum.177
  239.7 20.9 %all-reduce.1 = (f32[256,48]{0,1:T(8,128)S(1)}, f32[48]{0:T(128)S(1)}) all-reduce(f32[256,48]{0,1:T(8,128)S(1)} %convolution_bitcast_fusion.3, f32[48]{0:T(128)S(1)} %get-tuple-element.32), channel_id=1, replica_groups=mesh['row_0'=8,'row_1'=4,'feat_0'=4,'feat_1'=2] {'row_0'}, use_global_device_ids=true, to_apply=%region_24.0 | all-reduce | flops 12336 | bytes 98688 | tf_op jit(solution)/shard_map/psum | solution.py:45
  260.6 11.3 %all-reduce.7 = (f32[256,48]{0,1:T(8,128)S(1)}, f32[48]{0:T(128)S(1)}) all-reduce(f32[256,48]{0,1:T(8,128)S(1)} %get-tuple-element.4, f32[48]{0:T(128)S(1)} %get-tuple-element.5), channel_id=1, replica_groups=mesh['row_0'=8,'row_1'=4,'feat_0'=4,'feat_1'=2] {'row_1'}, use_global_device_ids=true, to_apply=%region_25.0 | all-reduce | flops 12336 | bytes 98688 | tf_op jit(solution)/shard_map/psum | solution.py:45
  272.0 12.1 %all-reduce.4 = (f32[256,48]{0,1:T(8,128)S(1)}, f32[48]{0:T(128)S(1)}) all-reduce(f32[256,48]{0,1:T(8,128)S(1)} %get-tuple-element.16, f32[48]{0:T(128)S(1)} %get-tuple-element.17), channel_id=1, replica_groups=mesh['row_0'=8,'row_1'=4,'feat_0'=4,'feat_1'=2] {'feat_0'}, use_global_device_ids=true, to_apply=%region_26.0 | all-reduce | flops 12336 | bytes 98688 | tf_op jit(solution)/shard_map/psum | solution.py:45
  284.0 17.8 %all-reduce.10 = (f32[256,48]{0,1:T(8,128)S(1)}, f32[48]{0:T(128)S(1)}) all-reduce(f32[256,48]{0,1:T(8,128)S(1)} %get-tuple-element.10, f32[48]{0:T(128)S(1)} %get-tuple-element.11), channel_id=1, replica_groups=mesh['row_0'=8,'row_1'=4,'feat_0'=4,'feat_1'=2] {'feat_1'}, use_global_device_ids=true, to_apply=%region_27.0 | all-reduce | flops 12336 | bytes 98688 | tf_op jit(solution)/shard_map/psum | solution.py:45
  302.0 0.5 multiply_reduce_fusion.2
  302.5 28.4 %all_to_all.53 = bf16[32,256,48]{1,2,0:T(8,128)(2,1)S(1)} all-to-all(bf16[32,256,48]{1,2,0:T(8,128)(2,1)S(1)} %broadcast_in_dim.14), channel_id=1, replica_groups=mesh['row_0'=8,'row_1'=4,'feat_0'=4,'feat_1'=2] {'row_0','row_1'}, dimensions={0} | all-to-all | bytes 1572864 | tf_op jit(solution)/shard_map/all_to_all | solution.py:34
  331.0 0.8 convolution_bitcast_fusion.7
  331.8 10.6 %all_to_all.54 = f32[8,128,48]{1,2,0:T(8,128)S(1)} all-to-all(f32[8,128,48]{1,2,0:T(8,128)S(1)} %broadcast_in_dim.15), channel_id=1, replica_groups=mesh['row_0'=8,'row_1'=4,'feat_0'=4,'feat_1'=2] {'feat_0','feat_1'}, dimensions={0} | all-to-all | bytes 393216 | tf_op jit(solution)/shard_map/all_to_all | solution.py:34
  342.8 1.4 copy.43
  344.2 5.0 all-to-all-start.6
  349.4 41.9 %psum.272 = f32[48]{0:T(128)S(1)} all-reduce(f32[48]{0:T(128)S(1)} %multiply_add_fusion.2), channel_id=1, replica_groups=mesh['row_0'=8,'row_1'=4,'feat_0'=4,'feat_1'=2] {'row_0'}, use_global_device_ids=true, to_apply=%region_32.0 | all-reduce | flops 48 | bytes 384 | tf_op jit(solution)/shard_map/psum | solution.py:45
  391.3 9.2 %psum.273 = f32[48]{0:T(128)S(1)} all-reduce(f32[48]{0:T(128)S(1)} %psum.272), channel_id=1, replica_groups=mesh['row_0'=8,'row_1'=4,'feat_0'=4,'feat_1'=2] {'row_1'}, use_global_device_ids=true, to_apply=%region_33.0 | all-reduce | flops 48 | bytes 384 | tf_op jit(solution)/shard_map/psum | solution.py:45
  400.5 6.9 %psum.274 = f32[48]{0:T(128)S(1)} all-reduce(f32[48]{0:T(128)S(1)} %psum.273), channel_id=1, replica_groups=mesh['row_0'=8,'row_1'=4,'feat_0'=4,'feat_1'=2] {'feat_0'}, use_global_device_ids=true, to_apply=%region_34.0 | all-reduce | flops 48 | bytes 384 | tf_op jit(solution)/shard_map/psum | solution.py:45
  407.3 10.3 %psum.275 = f32[48]{0:T(128)S(1)} all-reduce(f32[48]{0:T(128)S(1)} %psum.274), channel_id=1, replica_groups=mesh['row_0'=8,'row_1'=4,'feat_0'=4,'feat_1'=2] {'feat_1'}, use_global_device_ids=true, to_apply=%region_35.0 | all-reduce | flops 48 | bytes 384 | tf_op jit(solution)/shard_map/psum | solution.py:45
  417.7 1.5 reduce_sum.183
  419.6 20.9 %all-reduce = (f32[256,48]{0,1:T(8,128)S(1)}, f32[48]{0:T(128)S(1)}) all-reduce(f32[256,48]{0,1:T(8,128)S(1)} %convolution_bitcast_fusion.1, f32[48]{0:T(128)S(1)} %get-tuple-element.28), channel_id=1, replica_groups=mesh['row_0'=8,'row_1'=4,'feat_0'=4,'feat_1'=2] {'row_0'}, use_global_device_ids=true, to_apply=%region_42.0 | all-reduce | flops 12336 | bytes 98688 | tf_op jit(solution)/shard_map/psum | solution.py:45
  440.6 11.3 %all-reduce.6 = (f32[256,48]{0,1:T(8,128)S(1)}, f32[48]{0:T(128)S(1)}) all-reduce(f32[256,48]{0,1:T(8,128)S(1)} %get-tuple-element.2, f32[48]{0:T(128)S(1)} %get-tuple-element.3), channel_id=1, replica_groups=mesh['row_0'=8,'row_1'=4,'feat_0'=4,'feat_1'=2] {'row_1'}, use_global_device_ids=true, to_apply=%region_43.0 | all-reduce | flops 12336 | bytes 98688 | tf_op jit(solution)/shard_map/psum | solution.py:45
  451.9 12.1 %all-reduce.3 = (f32[256,48]{0,1:T(8,128)S(1)}, f32[48]{0:T(128)S(1)}) all-reduce(f32[256,48]{0,1:T(8,128)S(1)} %get-tuple-element.14, f32[48]{0:T(128)S(1)} %get-tuple-element.15), channel_id=1, replica_groups=mesh['row_0'=8,'row_1'=4,'feat_0'=4,'feat_1'=2] {'feat_0'}, use_global_device_ids=true, to_apply=%region_44.0 | all-reduce | flops 12336 | bytes 98688 | tf_op jit(solution)/shard_map/psum | solution.py:45
  464.0 17.8 %all-reduce.9 = (f32[256,48]{0,1:T(8,128)S(1)}, f32[48]{0:T(128)S(1)}) all-reduce(f32[256,48]{0,1:T(8,128)S(1)} %get-tuple-element.8, f32[48]{0:T(128)S(1)} %get-tuple-element.9), channel_id=1, replica_groups=mesh['row_0'=8,'row_1'=4,'feat_0'=4,'feat_1'=2] {'feat_1'}, use_global_device_ids=true, to_apply=%region_45.0 | all-reduce | flops 12336 | bytes 98688 | tf_op jit(solution)/shard_map/psum | solution.py:45
  482.4 28.6 %all_to_all.55 = bf16[32,256,48]{1,2,0:T(8,128)(2,1)S(1)} all-to-all(bf16[32,256,48]{1,2,0:T(8,128)(2,1)S(1)} %broadcast_in_dim.16), channel_id=1, replica_groups=mesh['row_0'=8,'row_1'=4,'feat_0'=4,'feat_1'=2] {'row_0','row_1'}, dimensions={0} | all-to-all | bytes 1572864 | tf_op jit(solution)/shard_map/all_to_all | solution.py:34
  511.1 0.8 convolution_bitcast_fusion.6
  512.0 10.6 %all_to_all.56 = f32[8,128,48]{1,2,0:T(8,128)S(1)} all-to-all(f32[8,128,48]{1,2,0:T(8,128)S(1)} %broadcast_in_dim.17), channel_id=1, replica_groups=mesh['row_0'=8,'row_1'=4,'feat_0'=4,'feat_1'=2] {'feat_0','feat_1'}, dimensions={0} | all-to-all | bytes 393216 | tf_op jit(solution)/shard_map/all_to_all | solution.py:34
  523.0 1.4 copy.42
  524.3 5.0 all-to-all-start.9
  529.5 42.0 %psum.284 = f32[48]{0:T(128)S(1)} all-reduce(f32[48]{0:T(128)S(1)} %multiply_add_fusion.1), channel_id=1, replica_groups=mesh['row_0'=8,'row_1'=4,'feat_0'=4,'feat_1'=2] {'row_0'}, use_global_device_ids=true, to_apply=%region_50.0 | all-reduce | flops 48 | bytes 384 | tf_op jit(solution)/shard_map/psum | solution.py:45
  571.4 9.2 %psum.285 = f32[48]{0:T(128)S(1)} all-reduce(f32[48]{0:T(128)S(1)} %psum.284), channel_id=1, replica_groups=mesh['row_0'=8,'row_1'=4,'feat_0'=4,'feat_1'=2] {'row_1'}, use_global_device_ids=true, to_apply=%region_51.0 | all-reduce | flops 48 | bytes 384 | tf_op jit(solution)/shard_map/psum | solution.py:45
  580.6 6.9 %psum.286 = f32[48]{0:T(128)S(1)} all-reduce(f32[48]{0:T(128)S(1)} %psum.285), channel_id=1, replica_groups=mesh['row_0'=8,'row_1'=4,'feat_0'=4,'feat_1'=2] {'feat_0'}, use_global_device_ids=true, to_apply=%region_52.0 | all-reduce | flops 48 | bytes 384 | tf_op jit(solution)/shard_map/psum | solution.py:45
  587.5 10.3 %psum.287 = f32[48]{0:T(128)S(1)} all-reduce(f32[48]{0:T(128)S(1)} %psum.286), channel_id=1, replica_groups=mesh['row_0'=8,'row_1'=4,'feat_0'=4,'feat_1'=2] {'feat_1'}, use_global_device_ids=true, to_apply=%region_53.0 | all-reduce | flops 48 | bytes 384 | tf_op jit(solution)/shard_map/psum | solution.py:45
  597.8 1.5 reduce_sum.189
  599.3 0.7 multiply_subtract_fusion
  (48 shorter events, 4.7 us)
Async XLA Ops:
  0.6 1.6 copy-start
  3.6 52.2 %copy-start.1 = (f32[256,256]{1,0:T(8,128)S(1)}, f32[256,256]{1,0:T(8,128)}, u32[]{:S(2)}) copy-start(f32[256,256]{1,0:T(8,128)} %param.7) | copy-start | bytes 786436
  3.6 120.4 %copy-start.2 = (f32[256]{0:T(256)S(1)}, f32[256]{0:T(256)}, u32[]{:S(2)}) copy-start(f32[256]{0:T(256)} %param.8) | copy-start | bytes 3076
  164.1 5.5 copy-start.3
  164.1 73.6 %all-to-all-start.3 = ((f32[32,256,48]{1,2,0:T(8,128)}), f32[32,256,48]{1,2,0:T(8,128)}, u32[]{:S(2)}, u32[]{:S(2)}) async-start(f32[32,256,48]{1,2,0:T(8,128)} %bitcast.73), calls=%async_computation.3 | async-start | bytes 3145728 | tf_op jit(solution)/shard_map/all_to_all | solution.py:22
  344.2 73.5 %all-to-all-start.6 = ((f32[32,256,48]{1,2,0:T(8,128)}), f32[32,256,48]{1,2,0:T(8,128)}, u32[]{:S(2)}, u32[]{:S(2)}) async-start(f32[32,256,48]{1,2,0:T(8,128)} %bitcast.75), calls=%async_computation.6 | async-start | bytes 3145728 | tf_op jit(solution)/shard_map/all_to_all | solution.py:22
  524.3 73.5 %all-to-all-start.9 = ((f32[32,256,48]{1,2,0:T(8,128)}), f32[32,256,48]{1,2,0:T(8,128)}, u32[]{:S(2)}, u32[]{:S(2)}) async-start(f32[32,256,48]{1,2,0:T(8,128)} %bitcast.74), calls=%async_computation.9 | async-start | bytes 3145728 | tf_op jit(solution)/shard_map/all_to_all | solution.py:22
where the time goes:
time: 601 us; the launch traced here: 600 us
  blocking collectives  563 us (94%)
  starting transfers between devices  15.3 us (3%)
  other arithmetic  8.02 us (1%)
  matrix products  6.96 us (1%)
  local copies, waits for them, and re-layouts  6.25 us (1%)
    psum x24, blocking collectives, one_axis_at_a_time(): shard = lax.psum(shard, axis)  397 us
    all_to_all x6, blocking collectives, copy_for_each(): lax.all_to_all(jnp.broadcast_to(shard[None], (devices, *shard.shape)), ax...  115 us
    all_to_all x1, blocking collectives, summed_on_arrival(): lax.all_to_all(pieces, axis, split_axis=0, concat_axis=0, tiled=True)  50.7 us
    all_to_all x3, starting transfers between devices, summed_on_arrival(): lax.all_to_all(pieces, axis, split_axis=0, concat_axis=0, tiled=True)  15.3 us
  transfers between devices with their start and end apart: 3, of which 0 were waited for; matrix products, arithmetic and copies ran while one was open for 0% of the time, Pallas kernels for 0%

commit v1 on v0

v1 whole, which is shorter than its diff:
```python
import jax
import jax.numpy as jnp
from jax import lax
from jax.sharding import Mesh
from jax.sharding import PartitionSpec as P

ITERS = 3
ROW = ("zh", "zl", "y")
FEAT = ("x", "c")
OWN = ("zl", "y")
MANY = ("zl", "y", "x", "c")
N_OWN, N_MANY, N_ZH = 8, 64, 4
BF = jnp.bfloat16
F32 = jnp.float32


def exchange(pieces, axes):
    return lax.all_to_all(pieces, axes, 0, 0, tiled=True)


def spread(shard, axes, count):
    return exchange(jnp.broadcast_to(shard[None], (count, *shard.shape)), axes)


def high_low(value):
    high = lax.reduce_precision(value, 8, 7)
    return high, value - high


def to_tiles(array):
    rows, lanes = array.shape
    tiled = array.reshape(rows // 8, 8, lanes // 128, 128).transpose(0, 2, 1, 3)
    return tiled.reshape(rows * lanes // 1024, 8, 128)


def from_tiles(tiles, rows, lanes):
    tiled = tiles.reshape(rows // 8, lanes // 128, 8, 128).transpose(0, 2, 1, 3)
    return tiled.reshape(rows, lanes)


def mm(a, b):
    return jnp.dot(a.astype(BF), b.astype(BF), preferred_element_type=F32)


def mm_t(a, b):
    return lax.dot_general(
        a.astype(BF), b.astype(BF), (((1,), (1,)), ((), ())), preferred_element_type=F32
    )


def scalar_tile(first, second):
    rows = []
    for value in (first, second):
        rows.extend(high_low(value))
    block = jnp.stack(rows)
    return jnp.pad(block, ((0, 4), (0, 80)))[None]


def split_again(tile):
    total = tile[0::2] + tile[1::2]
    high, low = high_low(total)
    return jnp.stack([high, low], axis=1).reshape(8, 128)


def shards(design, targets, factor, weights, penalty):
    blocks = design.reshape(128, 4, 8, 256).transpose(2, 0, 1, 3).reshape(8, 128, 1024)
    goal = targets.T.reshape(6, 1024)
    goal = jnp.broadcast_to(jnp.pad(goal, ((0, 2), (0, 0)))[None], (8, 8, 1024))
    moved = exchange(jnp.concatenate([blocks, goal], axis=1), OWN)
    mat = moved[:, :128].reshape(1024, 1024)
    goal = moved[:, 128:134].reshape(8, 48, 128).transpose(1, 0, 2).reshape(48, 1024)
    fac = spread(factor.astype(BF), "zh", N_ZH).reshape(1024, 256)

    zh = lax.axis_index("zh")
    me = lax.axis_index(MANY)
    w = weights[None, :]

    def over_zh(rows, square):
        part = mm(rows, mat).astype(BF)
        high, low = high_low(square)
        extra = jnp.pad(jnp.stack([high, low], axis=1), ((0, 0), (0, 126))).astype(BF)
        arrived = spread(jnp.concatenate([part, extra], axis=1), "zh", N_ZH)
        total = arrived.astype(F32).sum(axis=0)
        return total[:, :1024], total[:, 1024] + total[:, 1025]

    def over_many(tiles, scalar_at):
        per = tiles.shape[0] // N_MANY
        pieces = tiles.reshape(N_MANY, per * 8, 128)
        total = exchange(pieces.astype(BF), MANY).astype(F32).sum(axis=0)
        head = jnp.where(me == scalar_at // per, split_again(total[:8]), total[:8])
        total = jnp.concatenate([head, total[8:]]) if per > 1 else head
        return spread(total.astype(BF), MANY, N_MANY).reshape(N_MANY * per, 8, 128).astype(F32)

    residual, unused = over_zh(goal, jnp.zeros((48,), F32))
    answer = jnp.zeros_like(residual)
    direction = residual
    for step_index in range(ITERS):
        first = step_index == 0
        image = mm_t(residual, mat)
        projected = mm(residual, fac)
        scal = scalar_tile(
            jnp.sum(residual * residual, axis=1), jnp.sum(residual * direction, axis=1)
        )
        tiles = jnp.concatenate([to_tiles(image), to_tiles(projected), jnp.zeros((3, 8, 128), F32)])
        if first:
            fac_t = fac.T
            cross = to_tiles(mm_t(fac_t, mat))
            gram = to_tiles(mm(fac_t, fac))
            everything = jnp.concatenate([scal, jnp.zeros((5, 8, 128), F32), tiles[:60], cross, gram[:62]])
            everything = lax.dynamic_update_slice(everything, gram[62:], (1, 0, 0))
            back = over_many(everything, 0)
            scal = back[0]
            image_p = back[6:66]
            cross = from_tiles(back[66:322], 256, 1024)
            gram = from_tiles(jnp.concatenate([back[322:384], back[1:3]]), 256, 256)
        else:
            back = over_many(jnp.concatenate([scal, tiles]), 0)
            scal = back[0]
            image_p = back[1:61]
        image = from_tiles(image_p[:48], 48, 1024)
        projected = from_tiles(image_p[48:60], 48, 256)
        rr = (scal[0] + scal[1])[:48]
        rd = (scal[2] + scal[3])[:48]

        scaled = w * projected
        inner_next = rr + jnp.sum(scaled * projected, axis=1)
        through = mm(scaled, gram)
        ss = rr + 2.0 * jnp.sum(scaled * projected, axis=1) + jnp.sum(scaled * through, axis=1)
        search = residual + mm_t(scaled, fac)
        row_search = image + mm(scaled, cross)
        if first:
            direction, row_values = search, row_search
            dd = ss
            seen = projected + through
        else:
            beta = inner_next / inner
            sd = rd + jnp.sum(scaled * seen, axis=1)
            dd = ss + 2.0 * beta * sd + beta * beta * dd
            seen = projected + through + beta[:, None] * seen
            direction = search + beta[:, None] * direction
            row_values = row_search + beta[:, None] * row_values
        inner = inner_next
        row_low = row_values.astype(BF)
        square = jnp.sum(row_values * row_low.astype(F32), axis=1)
        if step_index + 1 < ITERS:
            hess, curvature = over_zh(row_low, square)
            step = (inner / (curvature + penalty * dd))[:, None]
            answer = answer + step * direction
            residual = residual - step * (hess + penalty[:, None] * direction)
        else:
            part = mm(row_low, mat).astype(BF).reshape(48, 4, 256).transpose(1, 0, 2)
            high, low = high_low(square)
            extra = jnp.pad(jnp.stack([high, low], axis=1), ((0, 0), (0, 126))).astype(BF)
            extra = jnp.broadcast_to(extra[None], (4, 48, 128))
            total = exchange(jnp.concatenate([part, extra], axis=2), "zh").astype(F32).sum(axis=0)
            curvature = total[:, 256] + total[:, 257]
            step = (inner / (curvature + penalty * dd))[:, None]

            def own(array):
                return lax.dynamic_slice(array, (0, zh * 256), (48, 256))

            mine = own(direction)
            answer = own(answer) + step * mine
            residual = own(residual) - step * (total[:, :256] + penalty[:, None] * mine)
    return answer.T, residual.T


def solution(mesh):
    finer = Mesh(mesh.devices.reshape(4, 2, 4, 4, 2), ("zh", "zl", "y", "x", "c"))
    spec = P((*FEAT, *ROW), None)
    in_specs = (P(ROW, FEAT), P(ROW, None), spec, P(), P())
    return jax.shard_map(
        shards, mesh=finer, in_specs=in_specs, out_specs=(spec, spec), check_vma=False
    )
```

time: 601 us -> 272 us (0.45)
  blocking collectives: 563 us -> 63.5 us
  waiting for transfers between devices: 0.01 us -> 84.6 us
  starting transfers between devices: 15.3 us -> 50.2 us
  local copies, waits for them, and re-layouts: 6.25 us -> 28.1 us
  matrix products: 6.96 us -> 23.4 us
  other arithmetic: 8.02 us -> 18.1 us
    psum x24 -> x0, blocking collectives: 397 us -> none  [one_axis_at_a_time(): shard = lax.psum(shard, axis)]
    all_to_all x7 -> x4, blocking collectives: 166 us -> 63.5 us  [exchange(): return lax.all_to_all(pieces, axes, 0, 0, tiled=True)]
    all_to_all x3 -> x8, waiting for transfers between devices: 0.01 us -> 84.6 us  [exchange(): return lax.all_to_all(pieces, axes, 0, 0, tiled=True)]
    all_to_all x3 -> x8, starting transfers between devices: 15.3 us -> 50.2 us  [exchange(): return lax.all_to_all(pieces, axes, 0, 0, tiled=True)]
    dot_general x13 -> x21, matrix products: 6.96 us -> 23.4 us  [the longest x14 15.6 us: mm(): return jnp.dot(a.astype(BF), b.astype(BF), preferred_element_type=F32)]
  transfers between devices with their start and end apart: 3 -> 8, of which waited for: 0 -> 7; matrix products, arithmetic and copies ran while one was open for 0% -> 7% of each run, Pallas kernels for 0% -> 0%
where the time goes in v1:
time: 272 us; the launch traced here: 270 us
  waiting for transfers between devices  84.6 us (31%)
  blocking collectives  63.5 us (23%)
  starting transfers between devices  50.2 us (18%)
  local copies, waits for them, and re-layouts  28.1 us (10%)
  matrix products  23.4 us (9%)
  other arithmetic  18.1 us (7%)
    all_to_all x8, waiting for transfers between devices, exchange(): return lax.all_to_all(pieces, axes, 0, 0, tiled=True)  84.6 us
    all_to_all x4, blocking collectives, exchange(): return lax.all_to_all(pieces, axes, 0, 0, tiled=True)  63.5 us
    all_to_all x8, starting transfers between devices, exchange(): return lax.all_to_all(pieces, axes, 0, 0, tiled=True)  50.2 us
    dot_general x14, matrix products, mm(): return jnp.dot(a.astype(BF), b.astype(BF), preferred_element_type=F32)  15.6 us
    dot_general x7, matrix products, mm_t(): lax.dot_general(a.astype(BF), b.astype(BF), (((1,), (1,)), ((), ())), pre...  7.85 us
    unnamed x79, local copies, waits for them, and re-layouts  7.41 us
  transfers between devices with their start and end apart: 8, of which 7 were waited for; matrix products, arithmetic and copies ran while one was open for 7% of the time, Pallas kernels for 0%

profile of v1, /device:TPU:1, one launch (start us, length us, event | category | flops | bytes accessed | tf_op | source)
XLA Modules:
  0.0 269.6 jit_solution(17761622119595067121)
XLA Ops:
  1.4 2.2 copy.71
  3.6 2.2 copy.76
  5.7 3.2 %reshape.398 = bf16[8,128,1024]{2,1,0:T(8,128)(2,1)S(1)} reshape(bf16[8,128,4,256]{3,2,1,0:T(4,128)(2,1)} %bitcast.311) | data formatting | bytes 4194304 | tf_op jit(solution)/shard_map/reshape | solution.py:66
  9.0 1.7 pad_maximum_fusion
  10.7 6.5 %all-to-all-start = ((bf16[8,136,1024]{2,1,0:T(8,128)(2,1)}), bf16[8,136,1024]{2,1,0:T(8,128)(2,1)S(1)}, u32[]{:S(2)}, u32[]{:S(2)}) async-start(bf16[8,136,1024]{2,1,0:T(8,128)(2,1)} %pad_maximum_fusion), calls=%async_computation | async-start | bytes 4456448 | tf_op jit(solution)/shard_map/all_to_all | solution.py:18
  17.3 27.5 %all-to-all-done = bf16[8,136,1024]{2,1,0:T(8,128)(2,1)S(1)} async-done(((bf16[8,136,1024]{2,1,0:T(8,128)(2,1)}), bf16[8,136,1024]{2,1,0:T(8,128)(2,1)S(1)}, u32[]{:S(2)}, u32[]{:S(2)}) %all-to-all-start) | async-done | bytes 2228256 | tf_op jit(solution)/shard_map/all_to_all | solution.py:18
  45.6 7.3 %all-to-all-start.2 = ((bf16[4,256,256]{1,2,0:T(8,128)(2,1)}), bf16[4,256,256]{1,2,0:T(8,128)(2,1)S(1)}, u32[]{:S(2)}, u32[]{:S(2)}) async-start(bf16[4,256,256]{1,2,0:T(8,128)(2,1)} %broadcast_in_dim.32), calls=%async_computation.2 | async-start | bytes 1048576 | tf_op jit(solution)/shard_map/all_to_all | solution.py:18
  53.5 10.9 %all-to-all-done.2 = bf16[4,256,256]{1,2,0:T(8,128)(2,1)S(1)} async-done(((bf16[4,256,256]{1,2,0:T(8,128)(2,1)}), bf16[4,256,256]{1,2,0:T(8,128)(2,1)S(1)}, u32[]{:S(2)}, u32[]{:S(2)}) %all-to-all-start.2) | async-done | bytes 524320 | tf_op jit(solution)/shard_map/all_to_all | solution.py:18
  65.2 5.3 %all-to-all-start.1 = ((bf16[4,48,1152]{2,1,0:T(8,128)(2,1)}), bf16[4,48,1152]{2,1,0:T(8,128)(2,1)}, u32[]{:S(2)}, u32[]{:S(2)}) async-start(bf16[4,48,1152]{2,1,0:T(8,128)(2,1)} %broadcast_in_dim.29), calls=%async_computation.1 | async-start | bytes 884736 | tf_op jit(solution)/shard_map/all_to_all | solution.py:18
  72.8 1.3 copy-done
  74.1 1.5 convolution_bitcast_fusion
  75.6 2.1 copy.55
  77.7 1.1 copy.77
  78.8 0.9 copy.56
  79.7 1.1 convert_reduce_fusion.3
  83.8 15.1 %all-to-all-start.3 = ((bf16[64,48,128]{2,1,0:T(8,128)(2,1)}), bf16[64,48,128]{2,1,0:T(8,128)(2,1)}, u32[]{:S(2)}, u32[]{:S(2)}) async-start(bf16[64,48,128]{2,1,0:T(8,128)(2,1)} %bitcast.329), calls=%async_computation.3 | async-start | bytes 1572864 | tf_op jit(solution)/shard_map/all_to_all | solution.py:18
  99.0 14.6 %all-to-all-done.3 = bf16[64,48,128]{2,1,0:T(8,128)(2,1)} async-done(((bf16[64,48,128]{2,1,0:T(8,128)(2,1)}), bf16[64,48,128]{2,1,0:T(8,128)(2,1)}, u32[]{:S(2)}, u32[]{:S(2)}) %all-to-all-start.3) | async-done | bytes 786464 | tf_op jit(solution)/shard_map/all_to_all | solution.py:18
  113.6 1.3 convert_reduce_fusion
  115.1 19.4 %all_to_all.60 = bf16[64,48,128]{2,1,0:T(8,128)(2,1)S(1)} all-to-all(bf16[64,48,128]{2,1,0:T(8,128)(2,1)S(1)} %broadcast_in_dim.33), channel_id=1, replica_groups=mesh['zh'=4,'zl'=2,'y'=4,'x'=4,'c'=2] {'zl','y','x','c'}, dimensions={0} | all-to-all | bytes 1572864 | tf_op jit(solution)/shard_map/all_to_all | solution.py:18
  136.2 1.0 multiply_reduce_fusion.6
  138.0 2.2 convolution_convert_fusion.2
  141.0 4.1 %all-to-all-start.5 = ((bf16[4,48,1152]{2,1,0:T(8,128)(2,1)}), bf16[4,48,1152]{2,1,0:T(8,128)(2,1)}, u32[]{:S(2)}, u32[]{:S(2)}) async-start(bf16[4,48,1152]{2,1,0:T(8,128)(2,1)} %broadcast_in_dim.34), calls=%async_computation.5 | async-start | bytes 884736 | tf_op jit(solution)/shard_map/all_to_all | solution.py:18
  145.8 1.6 slice.265
  147.3 1.3 reduce_sum.250
  148.7 0.9 pad_maximum_fusion.2
  149.6 1.3 slice_add_fusion.10
  150.9 2.2 multiply_reduce_fusion.11
  153.1 5.2 %all-to-all-done.5 = bf16[4,48,1152]{2,1,0:T(8,128)(2,1)} async-done(((bf16[4,48,1152]{2,1,0:T(8,128)(2,1)}), bf16[4,48,1152]{2,1,0:T(8,128)(2,1)}, u32[]{:S(2)}, u32[]{:S(2)}) %all-to-all-start.5) | async-done | bytes 442400 | tf_op jit(solution)/shard_map/all_to_all | solution.py:18
  158.3 1.1 convert_reduce_fusion.2
  160.2 1.8 multiply_reduce_fusion.5
  163.7 15.6 %all_to_all.61 = bf16[64,8,128]{2,1,0:T(8,128)(2,1)S(1)} all-to-all(bf16[64,8,128]{2,1,0:T(8,128)(2,1)S(1)} %maximum_maximum_fusion), channel_id=1, replica_groups=mesh['zh'=4,'zl'=2,'y'=4,'x'=4,'c'=2] {'zl','y','x','c'}, dimensions={0} | all-to-all | bytes 262144 | tf_op jit(solution)/shard_map/all_to_all | solution.py:18
  179.4 12.8 %all_to_all.62 = bf16[64,8,128]{2,1,0:T(8,128)(2,1)S(1)} all-to-all(bf16[64,8,128]{2,1,0:T(8,128)(2,1)S(1)} %broadcast_in_dim.36), channel_id=1, replica_groups=mesh['zh'=4,'zl'=2,'y'=4,'x'=4,'c'=2] {'zl','y','x','c'}, dimensions={0} | all-to-all | bytes 262144 | tf_op jit(solution)/shard_map/all_to_all | solution.py:18
  193.1 2.1 multiply_reduce_fusion.3
  196.0 2.2 convolution_convert_fusion.1
  199.0 4.1 %all-to-all-start.8 = ((bf16[4,48,1152]{2,1,0:T(8,128)(2,1)}), bf16[4,48,1152]{2,1,0:T(8,128)(2,1)}, u32[]{:S(2)}, u32[]{:S(2)}) async-start(bf16[4,48,1152]{2,1,0:T(8,128)(2,1)} %broadcast_in_dim.37), calls=%async_computation.8 | async-start | bytes 884736 | tf_op jit(solution)/shard_map/all_to_all | solution.py:18
  203.2 2.3 multiply_reduce_fusion.10
  205.5 10.7 %all-to-all-done.8 = bf16[4,48,1152]{2,1,0:T(8,128)(2,1)} async-done(((bf16[4,48,1152]{2,1,0:T(8,128)(2,1)}), bf16[4,48,1152]{2,1,0:T(8,128)(2,1)}, u32[]{:S(2)}, u32[]{:S(2)}) %all-to-all-start.8) | async-done | bytes 442400 | tf_op jit(solution)/shard_map/all_to_all | solution.py:18
  216.2 1.1 convert_reduce_fusion.1
  217.4 1.3 add_divide_fusion.1
  218.7 2.0 multiply_reduce_fusion.2
  222.1 15.7 %all_to_all.63 = bf16[64,8,128]{2,1,0:T(8,128)(2,1)S(1)} all-to-all(bf16[64,8,128]{2,1,0:T(8,128)(2,1)S(1)} %maximum_maximum_fusion.1), channel_id=1, replica_groups=mesh['zh'=4,'zl'=2,'y'=4,'x'=4,'c'=2] {'zl','y','x','c'}, dimensions={0} | all-to-all | bytes 262144 | tf_op jit(solution)/shard_map/all_to_all | solution.py:18
  238.6 4.4 %all-to-all-start.10 = ((bf16[64,8,128]{2,1,0:T(8,128)(2,1)}), bf16[64,8,128]{2,1,0:T(8,128)(2,1)S(1)}, u32[]{:S(2)}, u32[]{:S(2)}) async-start(bf16[64,8,128]{2,1,0:T(8,128)(2,1)} %broadcast_in_dim.39), calls=%async_computation.10 | async-start | bytes 262144 | tf_op jit(solution)/shard_map/all_to_all | solution.py:18
  243.0 8.6 %all-to-all-done.10 = bf16[64,8,128]{2,1,0:T(8,128)(2,1)S(1)} async-done(((bf16[64,8,128]{2,1,0:T(8,128)(2,1)}), bf16[64,8,128]{2,1,0:T(8,128)(2,1)S(1)}, u32[]{:S(2)}, u32[]{:S(2)}) %all-to-all-start.10) | async-done | bytes 131104 | tf_op jit(solution)/shard_map/all_to_all | solution.py:18
  251.7 1.6 multiply_reduce_fusion.8
  254.4 1.2 multiply_reduce_fusion
  257.0 3.3 %all-to-all-start.11 = ((bf16[4,48,384]{2,1,0:T(8,128)(2,1)}), bf16[4,48,384]{2,1,0:T(8,128)(2,1)S(1)}, u32[]{:S(2)}, u32[]{:S(2)}) async-start(bf16[4,48,384]{2,1,0:T(8,128)(2,1)} %pad_maximum_fusion.1), calls=%async_computation.11 | async-start | bytes 294912 | tf_op jit(solution)/shard_map/all_to_all | solution.py:18
  260.6 7.1 %all-to-all-done.11 = bf16[4,48,384]{2,1,0:T(8,128)(2,1)S(1)} async-done(((bf16[4,48,384]{2,1,0:T(8,128)(2,1)}), bf16[4,48,384]{2,1,0:T(8,128)(2,1)S(1)}, u32[]{:S(2)}, u32[]{:S(2)}) %all-to-all-start.11) | async-done | bytes 147488 | tf_op jit(solution)/shard_map/all_to_all | solution.py:18
  268.0 1.6 fusion.37
  (186 shorter events, 22.2 us)
Async XLA Ops:
  10.7 6.5 %copy-start.17 = (f32[256,256]{1,0:T(8,128)S(1)}, f32[256,256]{1,0:T(8,128)}, u32[]{:S(2)}) copy-start(f32[256,256]{1,0:T(8,128)} %param.7) | copy-start | bytes 786436
  10.7 34.1 %all-to-all-start = ((bf16[8,136,1024]{2,1,0:T(8,128)(2,1)}), bf16[8,136,1024]{2,1,0:T(8,128)(2,1)S(1)}, u32[]{:S(2)}, u32[]{:S(2)}) async-start(bf16[8,136,1024]{2,1,0:T(8,128)(2,1)} %pad_maximum_fusion), calls=%async_computation | async-start | bytes 4456448 | tf_op jit(solution)/shard_map/all_to_all | solution.py:18
  45.6 18.8 %all-to-all-start.2 = ((bf16[4,256,256]{1,2,0:T(8,128)(2,1)}), bf16[4,256,256]{1,2,0:T(8,128)(2,1)S(1)}, u32[]{:S(2)}, u32[]{:S(2)}) async-start(bf16[4,256,256]{1,2,0:T(8,128)(2,1)} %broadcast_in_dim.32), calls=%async_computation.2 | async-start | bytes 1048576 | tf_op jit(solution)/shard_map/all_to_all | solution.py:18
  65.2 14.5 %all-to-all-start.1 = ((bf16[4,48,1152]{2,1,0:T(8,128)(2,1)}), bf16[4,48,1152]{2,1,0:T(8,128)(2,1)}, u32[]{:S(2)}, u32[]{:S(2)}) async-start(bf16[4,48,1152]{2,1,0:T(8,128)(2,1)} %broadcast_in_dim.29), calls=%async_computation.1 | async-start | bytes 884736 | tf_op jit(solution)/shard_map/all_to_all | solution.py:18
  71.3 0.7 copy-start.14
  72.8 1.3 copy-start
  79.7 2.4 copy-start.8
  81.0 1.2 copy-start.15
  82.9 0.9 copy-start.12
  83.8 29.8 %all-to-all-start.3 = ((bf16[64,48,128]{2,1,0:T(8,128)(2,1)}), bf16[64,48,128]{2,1,0:T(8,128)(2,1)}, u32[]{:S(2)}, u32[]{:S(2)}) async-start(bf16[64,48,128]{2,1,0:T(8,128)(2,1)} %bitcast.329), calls=%async_computation.3 | async-start | bytes 1572864 | tf_op jit(solution)/shard_map/all_to_all | solution.py:18
  134.7 2.5 copy-start.4
  134.7 0.7 copy-start.18
  134.8 2.4 copy-start.7
  134.8 1.4 copy-start.2
  136.2 1.1 copy-start.16
  137.9 2.2 copy-start.19
  138.0 10.7 %slice-start = ((bf16[384,8,128]{2,1,0:T(8,128)(2,1)}), bf16[2,8,128]{2,1,0:T(8,128)(2,1)S(1)}, s32[]{:S(2)}) async-start(bf16[384,8,128]{2,1,0:T(8,128)(2,1)} %copy-done.7), calls=%async_computation.12 | async-start | bytes 8192 | tf_op jit(solution)/shard_map/slice | solution.py:115
  141.0 17.3 %all-to-all-start.5 = ((bf16[4,48,1152]{2,1,0:T(8,128)(2,1)}), bf16[4,48,1152]{2,1,0:T(8,128)(2,1)}, u32[]{:S(2)}, u32[]{:S(2)}) async-start(bf16[4,48,1152]{2,1,0:T(8,128)(2,1)} %broadcast_in_dim.34), calls=%async_computation.5 | async-start | bytes 884736 | tf_op jit(solution)/shard_map/all_to_all | solution.py:18
  149.6 1.3 copy-start.9
  160.2 3.3 %copy-start.27 = (f32[48]{0:T(128)}, f32[48]{0:T(128)S(1)}, u32[]{:S(2)}) copy-start(f32[48]{0:T(128)S(1)} %add_divide_fusion.2) | copy-start | bytes 580
  160.2 3.3 %copy-start.32 = (bf16[64]{0:T(256)(128)(2,1)S(1)}, bf16[64]{0:T(256)(128)(2,1)}, u32[]{:S(2)}) copy-start(bf16[64]{0:T(256)(128)(2,1)} %pad.62.clone) | copy-start | bytes 388
  162.1 0.7 copy-start.5
  162.4 30.7 %copy-start.26 = (f32[48]{0:T(128)S(1)}, f32[48]{0:T(128)}, u32[]{:S(2)}) copy-start(f32[48]{0:T(128)} %reduce_sum.250) | copy-start | bytes 580
  162.4 30.7 %copy-start.31 = (f32[1,1,128]{2,1,0:T(1,128)S(1)}, f32[1,1,128]{2,1,0:T(1,128)}, u32[]{:S(2)}) copy-start(f32[1,1,128]{2,1,0:T(1,128)} %slice_add_fusion.10) | copy-start | bytes 1540
  192.3 3.7 %copy-start.13 = (f32[12,8,128]{2,1,0:T(8,128)}, f32[12,8,128]{2,1,0:T(8,128)S(1)}, u32[]{:S(2)}) copy-start(f32[12,8,128]{2,1,0:T(8,128)S(1)} %slice.270) | copy-start | bytes 147460
  192.4 3.5 %copy-start.24 = (f32[48]{0:T(128)}, f32[48]{0:T(128)S(1)}, u32[]{:S(2)}) copy-start(f32[48]{0:T(128)S(1)} %reduce_sum.261) | copy-start | bytes 580
  193.1 2.9 %copy-start.25 = (f32[1,1,128]{2,1,0:T(1,128)}, f32[1,1,128]{2,1,0:T(1,128)S(1)}, u32[]{:S(2)}) copy-start(f32[1,1,128]{2,1,0:T(1,128)S(1)} %get-tuple-element.17) | copy-start | bytes 1540
  193.1 2.9 %copy-start.22 = (f32[48]{0:T(128)}, f32[48]{0:T(128)S(1)}, u32[]{:S(2)}) copy-start(f32[48]{0:T(128)S(1)} %fusion.105) | copy-start | bytes 580
  195.9 2.3 copy-start.20
  195.9 21.5 %copy-start.21 = (f32[48]{0:T(128)S(1)}, f32[48]{0:T(128)}, u32[]{:S(2)}) copy-start(f32[48]{0:T(128)} %param.9) | copy-start | bytes 580
  196.0 22.8 %copy-start.6 = (f32[48,1024]{1,0:T(8,128)S(1)}, f32[48,1024]{1,0:T(8,128)}, u32[]{:S(2)}) copy-start(f32[48,1024]{1,0:T(8,128)} %copy-done.5) | copy-start | bytes 589828
  199.0 17.1 %all-to-all-start.8 = ((bf16[4,48,1152]{2,1,0:T(8,128)(2,1)}), bf16[4,48,1152]{2,1,0:T(8,128)(2,1)}, u32[]{:S(2)}, u32[]{:S(2)}) async-start(bf16[4,48,1152]{2,1,0:T(8,128)(2,1)} %broadcast_in_dim.37), calls=%async_computation.8 | async-start | bytes 884736 | tf_op jit(solution)/shard_map/all_to_all | solution.py:18
  218.7 2.4 copy-start.29
  218.7 3.2 %copy-start.33 = (bf16[64]{0:T(256)(128)(2,1)S(1)}, bf16[64]{0:T(256)(128)(2,1)}, u32[]{:S(2)}) copy-start(bf16[64]{0:T(256)(128)(2,1)} %pad.62.clone) | copy-start | bytes 388
  220.8 1.1 copy-start.11
  220.8 30.9 %copy-start.23 = (f32[48]{0:T(128)S(1)}, f32[48]{0:T(128)}, u32[]{:S(2)}) copy-start(f32[48]{0:T(128)} %copy-done.22) | copy-start | bytes 580
  221.1 32.2 %copy-start.10 = (bf16[64,8,128]{2,1,0:T(8,128)(2,1)S(1)}, bf16[64,8,128]{2,1,0:T(8,128)(2,1)}, u32[]{:S(2)}) copy-start(bf16[64,8,128]{2,1,0:T(8,128)(2,1)} %copy-done.9) | copy-start | bytes 393220
  221.1 33.2 %copy-start.3 = (bf16[256,8,128]{2,1,0:T(8,128)(2,1)S(1)}, bf16[256,8,128]{2,1,0:T(8,128)(2,1)}, u32[]{:S(2)}) copy-start(bf16[256,8,128]{2,1,0:T(8,128)(2,1)} %copy-done.2) | copy-start | bytes 1572868
  221.9 33.7 %copy-start.1 = (bf16[8,128,1024]{2,1,0:T(8,128)(2,1)S(1)}, bf16[8,128,1024]{2,1,0:T(8,128)(2,1)}, u32[]{:S(2)}) copy-start(bf16[8,128,1024]{2,1,0:T(8,128)(2,1)} %copy-done) | copy-start | bytes 6291460
  238.6 13.0 %all-to-all-start.10 = ((bf16[64,8,128]{2,1,0:T(8,128)(2,1)}), bf16[64,8,128]{2,1,0:T(8,128)(2,1)S(1)}, u32[]{:S(2)}, u32[]{:S(2)}) async-start(bf16[64,8,128]{2,1,0:T(8,128)(2,1)} %broadcast_in_dim.39), calls=%async_computation.10 | async-start | bytes 262144 | tf_op jit(solution)/shard_map/all_to_all | solution.py:18
  255.6 12.3 %copy-start.34 = (f32[48]{0:T(128)S(1)}, f32[48]{0:T(128)}, u32[]{:S(2)}) copy-start(f32[48]{0:T(128)} %multiply_reduce_fusion.8) | copy-start | bytes 580
  255.6 12.3 %copy-start.35 = (f32[48]{0:T(128)S(1)}, f32[48]{0:T(128)}, u32[]{:S(2)}) copy-start(f32[48]{0:T(128)} %get-tuple-element.10) | copy-start | bytes 580
  255.6 12.3 %copy-start.28 = (f32[48]{0:T(128)S(1)}, f32[48]{0:T(128)}, u32[]{:S(2)}) copy-start(f32[48]{0:T(128)} %copy-done.27) | copy-start | bytes 580
  255.7 12.3 %copy-start.30 = (f32[48]{0:T(128)S(1)}, f32[48]{0:T(128)}, u32[]{:S(2)}) copy-start(f32[48]{0:T(128)} %copy-done.29) | copy-start | bytes 580
  257.0 10.7 %all-to-all-start.11 = ((bf16[4,48,384]{2,1,0:T(8,128)(2,1)}), bf16[4,48,384]{2,1,0:T(8,128)(2,1)S(1)}, u32[]{:S(2)}, u32[]{:S(2)}) async-start(bf16[4,48,384]{2,1,0:T(8,128)(2,1)} %pad_maximum_fusion.1), calls=%async_computation.11 | async-start | bytes 294912 | tf_op jit(solution)/shard_map/all_to_all | solution.py:18

commit v2 on v0

v2 whole, which is shorter than its diff:
```python
import jax
import jax.numpy as jnp
from jax import lax
from jax.experimental import pallas as pl
from jax.experimental.pallas import tpu as pltpu
from jax.sharding import Mesh
from jax.sharding import PartitionSpec as P

ITERS = 3
ROW = ("zh", "zl", "y")
FEAT = ("x", "c")
OWN = ("zl", "y")
MANY = ("zl", "y", "x", "c")
N_OWN, N_MANY, N_ZH = 8, 64, 4
T, RANK, BLOCK = 48, 256, 1024
SCAL = 480
HEAD = 512
BF = jnp.bfloat16
F32 = jnp.float32


def exchange(pieces, axes):
    return lax.all_to_all(pieces, axes, 0, 0, tiled=True)


def spread(shard, axes, count):
    return exchange(jnp.broadcast_to(shard[None], (count, *shard.shape)), axes)


def high_low(value):
    high = lax.reduce_precision(value, 8, 7)
    return high, value - high


def dot(a, b):
    return jnp.dot(a, b, preferred_element_type=F32)


def dot_t(a, b):
    return lax.dot_general(a, b, (((1,), (1,)), ((), ())), preferred_element_type=F32)


def call(body, out, **kw):
    return pl.pallas_call(body, out_shape=out, **kw)


def shape(*dims, dtype=F32):
    return jax.ShapeDtypeStruct(dims, dtype)


def columns(parts):
    lane = lax.broadcasted_iota(jnp.int32, (T, 128), 1)
    block = jnp.zeros((T, 128), F32)
    for index, part in enumerate(parts):
        block = jnp.where(lane == index, part, block)
    return block


def split16(value):
    high = value.astype(BF).astype(F32)
    return high, value - high


def total_of(array):
    return jnp.sum(array, axis=1, keepdims=True)


def pack_kernel(a0, a1, a2, a3, goal, out):
    for index, block in enumerate((a0, a1, a2, a3)):
        out[0, :128, index * 256 : (index + 1) * 256] = block[...]
    for index in range(6):
        out[0, 128:136, index * 128 : (index + 1) * 128] = goal[index * 8 : index * 8 + 8, :]
    out[0, 128:136, 768:] = jnp.zeros((8, 256), BF)


def pack(design, goal):
    def part(index):
        return pl.BlockSpec((128, 256), lambda s, index=index: (0, index * 8 + s))

    return pl.pallas_call(
        pack_kernel,
        grid=(8,),
        in_specs=[part(0), part(1), part(2), part(3), pl.BlockSpec((T, 128), lambda s: (0, 0))],
        out_specs=pl.BlockSpec((1, 136, BLOCK), lambda s: (s, 0, 0)),
        out_shape=shape(8, 136, BLOCK, dtype=BF),
    )(design, design, design, design, goal)


def start_kernel(mat, out):
    part = jnp.zeros((T, BLOCK), F32)
    for src in range(8):
        goal = jnp.concatenate(
            [mat[src, 128:136, t * 128 : (t + 1) * 128].astype(F32) for t in range(6)], axis=0
        ).astype(BF)
        part = part + dot(goal, mat[src, :128, :])
    high, low = split16(part)
    high, low = high.astype(BF), low.astype(BF)
    for to in range(N_ZH):
        out[to, :, :BLOCK] = high
        out[to, :, BLOCK:] = low[:, to * 256 : (to + 1) * 256]


def cross_kernel(mat, fac, gram, out):
    factor = fac[...]
    for src in range(8):
        block = dot(mat[src, :128, :], factor).astype(BF)
        out[src * 256 : src * 256 + 128, :] = block[:, :128]
        out[src * 256 + 128 : src * 256 + 256, :] = block[:, 128:]
    both = gram[...].astype(BF)
    out[2048:2304, :] = both[:, :128]
    out[2304:2560, :] = both[:, 128:]


def write_head(residual, direction, mat, fac, out):
    low = residual.astype(BF)
    for src in range(8):
        out[src * T : (src + 1) * T, :] = dot_t(low, mat[src, :128, :]).astype(BF)
    seen = dot(low, fac[...]).astype(BF)
    out[384:432, :] = seen[:, :128]
    out[432:480, :] = seen[:, 128:]
    rr = split16(total_of(residual * residual))
    rd = split16(total_of(residual * direction))
    block = jnp.concatenate([columns([*rr, *rd]), jnp.zeros((80, 128), F32)], axis=0)
    tile = block.T[:32, :]
    out[SCAL:HEAD, :] = tile.astype(BF)


def first_kernel(arrived, mat, fac, rest, out, residual_out, fix_out):
    residual = jnp.zeros((T, BLOCK), F32)
    fix = jnp.zeros((T, 256), F32)
    for source in range(N_ZH):
        residual = residual + arrived[source, :, :BLOCK].astype(F32)
        fix = fix + arrived[source, :, BLOCK:].astype(F32)
    residual_out[...] = residual
    fix_out[...] = fix
    write_head(residual, residual, mat, fac, out)
    out[HEAD:, :] = rest[...]


def next_kernel(
    arrived, direction_in, residual_in, answer_in, scal_in, penalty, mat, fac, out, residual_out, answer_out
):
    hess = jnp.zeros((T, BLOCK + 128), F32)
    for source in range(N_ZH):
        hess = hess + arrived[source].astype(F32)
    square = hess[:, BLOCK : BLOCK + 1] + hess[:, BLOCK + 1 : BLOCK + 2]
    hess = hess[:, :BLOCK]
    inner, dd = scal_in[:, :1], scal_in[:, 1:2]
    ridge = penalty[:, :1]
    direction = direction_in[...]
    step = inner / (square + ridge * dd)
    answer = step * direction
    if answer_in is not None:
        answer = answer_in[...] + answer
    answer_out[...] = answer
    residual = residual_in[...] - step * (hess + ridge * direction)
    residual_out[...] = residual
    write_head(residual, direction, mat, fac, out)


def search_kernel(first, last, *refs):
    refs = list(refs)
    back = refs.pop(0)
    full = back if first else refs.pop(0)
    mat, fac, weights, residual_in = refs[:4]
    refs = refs[4:]
    if not first:
        direction_in, row_in, seen_in, scal_in = refs[:4]
        refs = refs[4:]
    out, direction_out, row_out, seen_out, scal_out = refs

    scaled = weights[0:1, :]
    projected = jnp.concatenate([back[384:432, :], back[432:480, :]], axis=1).astype(F32)
    tile = jnp.concatenate([back[SCAL:HEAD, :].astype(F32), jnp.zeros((96, 128), F32)], axis=0).T
    rr = tile[:T, 0:1] + tile[:T, 1:2]
    rd = tile[:T, 2:3] + tile[:T, 3:4]
    scaled = scaled * projected
    cross_inner = total_of(scaled * projected)
    inner = rr + cross_inner
    low = scaled.astype(BF)
    through = jnp.concatenate([dot(low, full[2560:2816, :]), dot(low, full[2816:3072, :])], axis=1)
    dd = rr + 2.0 * cross_inner + total_of(scaled * through)
    seen = projected + through
    direction = residual_in[...] + dot_t(low, fac[...])
    if not first:
        before, dd_before = scal_in[:, :1], scal_in[:, 1:2]
        beta = inner / before
        sd = rd + total_of(scaled * seen_in[...])
        dd = dd + 2.0 * beta * sd + beta * beta * dd_before
        seen = seen + beta * seen_in[...]
        direction = direction + beta * direction_in[...]
    direction_out[...] = direction
    seen_out[...] = seen
    scal_out[...] = columns([inner, dd])
    part = jnp.zeros((T, BLOCK), F32)
    square = jnp.zeros((T, 1), F32)
    for src in range(8):
        at = HEAD + src * 256
        row = back[src * T : (src + 1) * T, :].astype(F32)
        row = row + dot_t(low[:, :128], full[at : at + 128, :])
        row = row + dot_t(low[:, 128:], full[at + 128 : at + 256, :])
        if not first:
            row = row + beta * row_in[:, src * 128 : (src + 1) * 128]
        row_out[:, src * 128 : (src + 1) * 128] = row
        row_low = row.astype(BF)
        square = square + total_of(row * row_low.astype(F32))
        part = part + dot(row_low, mat[src, :128, :])
    extra = columns(split16(square)).astype(BF)
    high, low = split16(part)
    high, low = high.astype(BF), low.astype(BF)
    for to in range(N_ZH):
        if last:
            mine = slice(to * 256, (to + 1) * 256)
            out[to, :, :256] = high[:, mine]
            out[to, :, 256:512] = low[:, mine]
            out[to, :, 512:] = extra
        else:
            out[to, :, :BLOCK] = high
            out[to, :, BLOCK:] = extra


def split_again(tile):
    total = tile[0:4:2] + tile[1:4:2]
    high, low = high_low(total)
    return jnp.concatenate([jnp.stack([high, low], axis=1).reshape(4, 128), tile[4:]])


def shards(design, targets, factor, weights, penalty):
    zh = lax.axis_index("zh")
    me = lax.axis_index(MANY)
    low_factor = factor.astype(BF)
    slots = jnp.zeros((N_ZH, 256, RANK), BF)
    slots = lax.dynamic_update_slice(slots, low_factor[None], (zh, 0, 0))
    for shift in range(1, N_ZH):
        pairs = [(i, (i + shift) % N_ZH) for i in range(N_ZH)]
        other = lax.ppermute(low_factor, "zh", pairs)
        slots = lax.dynamic_update_slice(slots, other[None], ((zh - shift) % N_ZH, 0, 0))
    fac = slots.reshape(BLOCK, RANK)

    mat = exchange(pack(design, targets.T), OWN)
    arrived = call(start_kernel, shape(N_ZH, T, BLOCK + 256, dtype=BF))(mat)
    arrived = exchange(arrived, "zh")
    gram = lax.dot_general(fac, fac, (((0,), (0,)), ((), ())), preferred_element_type=F32)
    rest = call(cross_kernel, shape(2560, 128, dtype=BF))(mat, fac, gram)

    w = jnp.broadcast_to(weights[None, :], (8, RANK))
    ridge = jnp.broadcast_to(penalty[:, None], (T, 128))

    def over_many(packed):
        pieces = packed.reshape(N_MANY, -1, 128)
        count = pieces.shape[1]
        total = exchange(pieces, MANY).astype(F32).sum(axis=0)
        head = jnp.where(me == SCAL // count, split_again(total[:8]), total[:8])
        if count > 8:
            head = jnp.concatenate([head, total[8:]])
        return spread(head.astype(BF), MANY, N_MANY).reshape(N_MANY * count, 128)

    packed, residual, fix = call(
        first_kernel,
        (shape(3072, 128, dtype=BF), shape(T, BLOCK), shape(T, 256)),
    )(arrived, mat, fac, rest)
    answer = None
    for step_index in range(ITERS):
        first, last = step_index == 0, step_index == ITERS - 1
        back = over_many(packed)
        if first:
            full = back
            state = ()
        else:
            state = (direction, row_values, seen, scal)
        args = (back,) if first else (back, full)
        wide = 640 if last else BLOCK + 128
        send, direction, row_values, seen, scal = call(
            lambda *refs, first=first, last=last: search_kernel(first, last, *refs),
            (
                shape(N_ZH, T, wide, dtype=BF),
                shape(T, BLOCK),
                shape(T, BLOCK),
                shape(T, RANK),
                shape(T, 128),
            ),
        )(*args, mat, fac, w, residual, *state)
        arrived = exchange(send, "zh")
        if last:
            break
        if answer is None:
            packed, residual, answer = call(
                lambda a, d, r, s, p, m, f, *outs: next_kernel(a, d, r, None, s, p, m, f, *outs),
                (shape(HEAD, 128, dtype=BF), shape(T, BLOCK), shape(T, BLOCK)),
            )(arrived, direction, residual, scal, ridge, mat, fac)
        else:
            packed, residual, answer = call(
                next_kernel,
                (shape(HEAD, 128, dtype=BF), shape(T, BLOCK), shape(T, BLOCK)),
            )(arrived, direction, residual, answer, scal, ridge, mat, fac)

    total = arrived.astype(F32).sum(axis=0)
    curvature = total[:, 512] + total[:, 513]
    step = (scal[:, 0] / (curvature + penalty * scal[:, 1]))[:, None]

    def own(array):
        return lax.dynamic_slice(array, (0, zh * 256), (T, 256))

    mine = own(direction)
    answer = own(answer) + step * mine
    hess = total[:, :256] + total[:, 256:512] + penalty[:, None] * mine
    residual = own(residual) + fix - step * hess
    return answer.T, residual.T


def solution(mesh):
    finer = Mesh(mesh.devices.reshape(4, 2, 4, 4, 2), ("zh", "zl", "y", "x", "c"))
    spec = P((*FEAT, *ROW), None)
    in_specs = (P(ROW, FEAT), P(ROW, None), spec, P(), P())
    return jax.shard_map(
        shards, mesh=finer, in_specs=in_specs, out_specs=(spec, spec), check_vma=False
    )
```

time: 601 us -> 247 us (0.41)
  blocking collectives: 563 us -> 96.6 us
  waiting for transfers between devices: 0.01 us -> 52.5 us
  Pallas kernels: 0 us -> 37.4 us
  starting transfers between devices: 15.3 us -> 47.6 us
    psum x24 -> x0, blocking collectives: 397 us -> none  [one_axis_at_a_time(): shard = lax.psum(shard, axis)]
    all_to_all x7 -> x6, blocking collectives: 166 us -> 96.6 us  [exchange(): return lax.all_to_all(pieces, axes, 0, 0, tiled=True)]
    all_to_all x3 -> x5, waiting for transfers between devices: 0.01 us -> 52.5 us  [exchange(): return lax.all_to_all(pieces, axes, 0, 0, tiled=True)]
    pallas_call x0 -> x9, Pallas kernels: none -> 37.4 us  [the longest x3 14 us: shards(): call(lambda *refs, first=first, last=last: search_kernel(first, last, *re...]
    all_to_all x3 -> x5, starting transfers between devices: 15.3 us -> 38 us  [exchange(): return lax.all_to_all(pieces, axes, 0, 0, tiled=True)]
    ppermute x0 -> x3, starting transfers between devices: none -> 9.67 us  [shards(): other = lax.ppermute(low_factor, 'zh', pairs)]
    reduce_sum x16 -> x4, other arithmetic: 7.22 us -> 0.31 us  [the longest x3 0.28 us: over_many(): total = exchange(pieces, MANY).astype(F32).sum(axis=0)]
  transfers between devices with their start and end apart: 3 -> 8, of which waited for: 0 -> 5; matrix products, arithmetic and copies ran while one was open for 0% -> 2% of each run, Pallas kernels for 0% -> 3%
where the time goes in v2:
time: 247 us; the launch traced here: 246 us
  blocking collectives  96.6 us (39%)
  waiting for transfers between devices  52.5 us (21%)
  starting transfers between devices  47.6 us (19%)
  Pallas kernels  37.4 us (15%)
  local copies, waits for them, and re-layouts  7.18 us (3%)
    all_to_all x6, blocking collectives, exchange(): return lax.all_to_all(pieces, axes, 0, 0, tiled=True)  96.6 us
    all_to_all x5, waiting for transfers between devices, exchange(): return lax.all_to_all(pieces, axes, 0, 0, tiled=True)  52.5 us
    all_to_all x5, starting transfers between devices, exchange(): return lax.all_to_all(pieces, axes, 0, 0, tiled=True)  38 us
    pallas_call x3, Pallas kernels, shards(): call(lambda *refs, first=first, last=last: search_kernel(first, last, *re...  14 us
    ppermute x3, starting transfers between devices, shards(): other = lax.ppermute(low_factor, 'zh', pairs)  9.67 us
    pallas_call x1, Pallas kernels, pack(): pl.pallas_call(pack_kernel, grid=(8,), in_specs=[part(0), part(1), part(2...  5.76 us
  transfers between devices with their start and end apart: 8, of which 5 were waited for; matrix products, arithmetic and copies ran while one was open for 2% of the time, Pallas kernels for 3%

profile of v2, /device:TPU:1, one launch (start us, length us, event | category | flops | bytes accessed | tf_op | source)
XLA Modules:
  0.0 245.6 jit_solution(16303117196329024332)
XLA Ops:
  0.6 5.8 %shard_map.68 = bf16[8,136,1024]{2,1,0:T(8,128)(2,1)} custom-call(bf16[128,8192]{1,0:T(8,128)(2,1)} %a3.1, bf16[128,8192]{1,0:T(8,128)(2,1)} %a3.1, bf16[128,8192]{1,0:T(8,128)(2,1)} %a3.1, bf16[128,8192]{1,0:T(8,128)(2,1)} %a3.1, bf16[48,128]{1,0:T(8,128)(2,1)} %bitcast.53), custom_call_target="tpu_custom_call" | custom-call | tf_op jit(solution)/shard_map/pallas_call | solution.py:80
  6.4 6.5 %all-to-all-start = ((bf16[8,136,1024]{2,1,0:T(8,128)(2,1)}), bf16[8,136,1024]{2,1,0:T(8,128)(2,1)S(1)}, u32[]{:S(2)}, u32[]{:S(2)}) async-start(bf16[8,136,1024]{2,1,0:T(8,128)(2,1)} %shard_map.68), calls=%async_computation | async-start | bytes 4456448 | tf_op jit(solution)/shard_map/all_to_all | solution.py:23
  12.9 6.1 %collective-permute-start.1 = (bf16[256,256]{1,0:T(8,128)(2,1)S(1)}, bf16[256,256]{1,0:T(8,128)(2,1)}, u32[]{:S(2)}, u32[]{:S(2)}) collective-permute-start(bf16[256,256]{1,0:T(8,128)(2,1)S(1)} %convert_element_type.34), channel_id=1, source_target_pairs={{0,128},{64,192},{128,0},{192,64},{1,129},{65,193},{129,1},{193,65... | collective-permute-start | bytes 393224 | tf_op jit(solution)/shard_map/ppermute | solution.py:236
  19.0 1.2 collective-permute-start
  20.2 2.4 collective-permute-start.2
  22.6 18.6 %all-to-all-done.mat.refs_1_.m.refs_2_ = bf16[8,136,1024]{2,1,0:T(8,128)(2,1)S(1)} async-done(((bf16[8,136,1024]{2,1,0:T(8,128)(2,1)}), bf16[8,136,1024]{2,1,0:T(8,128)(2,1)S(1)}, u32[]{:S(2)}, u32[]{:S(2)}) %all-to-all-start) | async-done | bytes 2228256 | tf_op jit(solution)/shard_map/all_to_all | solution.py:23
  41.2 1.4 copy-done
  42.6 2.8 %shard_map.69 = bf16[4,48,1280]{2,1,0:T(8,128)(2,1)} custom-call(bf16[8,136,1024]{2,1,0:T(8,128)(2,1)} %copy-done), custom_call_target="tpu_custom_call" | custom-call | tf_op jit(solution)/shard_map/pallas_call | solution.py:241
  45.4 7.9 %all-to-all-start.1 = ((bf16[4,48,1280]{2,1,0:T(8,128)(2,1)}), bf16[4,48,1280]{2,1,0:T(8,128)(2,1)S(1)}, u32[]{:S(2)}, u32[]{:S(2)}) async-start(bf16[4,48,1280]{2,1,0:T(8,128)(2,1)} %shard_map.69), calls=%async_computation.1 | async-start | bytes 983040 | tf_op jit(solution)/shard_map/all_to_all | solution.py:23
  53.4 0.1 copy.15
  53.6 0.0 collective-permute-done.1
  53.6 1.0 copy.17
  54.7 0.0 collective-permute-done
  54.7 0.1 copy.16
  54.8 0.0 collective-permute-done.2
  54.8 0.1 copy.18
  55.0 1.0 copy.19
  56.0 1.0 convolution_bitcast_fusion.gram
  57.0 3.4 %shard_map.70.rest = bf16[2560,128]{1,0:T(8,128)(2,1)} custom-call(bf16[8,136,1024]{2,1,0:T(8,128)(2,1)} %copy-done, bf16[1024,256]{1,0:T(8,128)(2,1)} %bitcast.36, f32[256,256]{1,0:T(8,128)} %convolution_bitcast_fusion.gram), custom_call_target="tpu_custom_call" | custom-call | tf_op jit(solution)/shard_map/pallas_call | solution.py:244
  60.4 3.0 %all-to-all-done.1.arrived = bf16[4,48,1280]{2,1,0:T(8,128)(2,1)S(1)} async-done(((bf16[4,48,1280]{2,1,0:T(8,128)(2,1)}), bf16[4,48,1280]{2,1,0:T(8,128)(2,1)S(1)}, u32[]{:S(2)}, u32[]{:S(2)}) %all-to-all-start.1) | async-done | bytes 491552 | tf_op jit(solution)/shard_map/all_to_all | solution.py:23
  63.3 0.8 copy-done.1
  64.1 3.8 %shard_map.71 = (bf16[3072,128]{1,0:T(8,128)(2,1)}, f32[48,1024]{1,0:T(8,128)}, f32[48,256]{1,0:T(8,128)}) custom-call(bf16[4,48,1280]{2,1,0:T(8,128)(2,1)} %copy-done.1, bf16[8,136,1024]{2,1,0:T(8,128)(2,1)} %copy-done, bf16[1024,256]{1,0:T(8,128)(2,1)} %bitcast.37, bf16[2560,128]{1,0:T(8,128)(2,1)} %shard_map.70.rest), custom_call_target="tpu_custom_call" | custom-call | tf_op jit(solution)/shard_map/pallas_call | solution.py:258
  68.0 14.3 %all-to-all-start.2 = ((bf16[64,48,128]{2,1,0:T(8,128)(2,1)}), bf16[64,48,128]{2,1,0:T(8,128)(2,1)S(1)}, u32[]{:S(2)}, u32[]{:S(2)}) async-start(bf16[64,48,128]{2,1,0:T(8,128)(2,1)} %bitcast.46), calls=%async_computation.2 | async-start | bytes 1572864 | tf_op jit(solution)/shard_map/all_to_all | solution.py:23
  82.4 14.7 %all-to-all-done.2 = bf16[64,48,128]{2,1,0:T(8,128)(2,1)S(1)} async-done(((bf16[64,48,128]{2,1,0:T(8,128)(2,1)}), bf16[64,48,128]{2,1,0:T(8,128)(2,1)S(1)}, u32[]{:S(2)}, u32[]{:S(2)}) %all-to-all-start.2) | async-done | bytes 786464 | tf_op jit(solution)/shard_map/all_to_all | solution.py:23
  97.1 0.1 convert_reduce_fusion
  97.3 0.1 broadcast_in_dim.25
  97.4 19.5 %all_to_all.55 = bf16[64,48,128]{2,1,0:T(8,128)(2,1)} all-to-all(bf16[64,48,128]{2,1,0:T(8,128)(2,1)S(1)} %broadcast_in_dim.25), channel_id=1, replica_groups=mesh['zh'=4,'zl'=2,'y'=4,'x'=4,'c'=2] {'zl','y','x','c'}, dimensions={0} | all-to-all | bytes 1572864 | tf_op jit(solution)/shard_map/all_to_all | solution.py:23
  117.0 0.6 broadcast_in_dim.26.refs_3_.refs_4_
  117.6 4.7 %shard_map.72 = (bf16[4,48,1152]{2,1,0:T(8,128)(2,1)}, f32[48,1024]{1,0:T(8,128)}, f32[48,1024]{1,0:T(8,128)}, f32[48,256]{1,0:T(8,128)}, f32[48,128]{1,0:T(8,128)}) custom-call(bf16[3072,128]{1,0:T(8,128)(2,1)} %bitcast.43, bf16[8,136,1024]{2,1,0:T(8,128)(2,1)} %copy-done, bf16[1024,256]{1,0:T(8,128)(2,1)} %bitcast.38, ...), custom_call_target="tpu_custom_call" | custom-call | tf_op jit(solution)/shard_map/pallas_call | solution.py:273
  122.3 18.8 %all_to_all.56.a = bf16[4,48,1152]{2,1,0:T(8,128)(2,1)} all-to-all(bf16[4,48,1152]{2,1,0:T(8,128)(2,1)} %get-tuple-element.26), channel_id=1, replica_groups=mesh['zh'=4,'zl'=2,'y'=4,'x'=4,'c'=2] {'zh'}, dimensions={0} | all-to-all | bytes 884736 | tf_op jit(solution)/shard_map/all_to_all | solution.py:23
  141.1 0.7 broadcast_in_dim.54.p.penalty
  141.8 3.7 %shard_map.73 = (bf16[512,128]{1,0:T(8,128)(2,1)}, f32[48,1024]{1,0:T(8,128)}, f32[48,1024]{1,0:T(8,128)}) custom-call(bf16[4,48,1152]{2,1,0:T(8,128)(2,1)} %all_to_all.56.a, f32[48,1024]{1,0:T(8,128)} %get-tuple-element.27.d.refs_6_, f32[48,1024]{1,0:T(8,128)} %get-tuple-element.25.refs_4_.r, f32[48,128]{1,0:T(8,128)} %get-tuple-element.28.s.refs_9_, ...), custom_call_target="tpu_custom_call" | custom-call | tf_op jit(solution)/shard_map/pallas_call | solution.py:287
  145.5 5.8 %all-to-all-start.5 = ((bf16[64,8,128]{2,1,0:T(8,128)(2,1)}), bf16[64,8,128]{2,1,0:T(8,128)(2,1)S(1)}, u32[]{:S(2)}, u32[]{:S(2)}) async-start(bf16[64,8,128]{2,1,0:T(8,128)(2,1)} %bitcast.51), calls=%async_computation.5 | async-start | bytes 262144 | tf_op jit(solution)/shard_map/all_to_all | solution.py:23
  151.3 8.5 %all-to-all-done.5 = bf16[64,8,128]{2,1,0:T(8,128)(2,1)S(1)} async-done(((bf16[64,8,128]{2,1,0:T(8,128)(2,1)}), bf16[64,8,128]{2,1,0:T(8,128)(2,1)S(1)}, u32[]{:S(2)}, u32[]{:S(2)}) %all-to-all-start.5) | async-done | bytes 131104 | tf_op jit(solution)/shard_map/all_to_all | solution.py:23
  159.8 0.1 convert_reduce_fusion.3
  160.0 12.9 %all_to_all.57 = bf16[64,8,128]{2,1,0:T(8,128)(2,1)} all-to-all(bf16[64,8,128]{2,1,0:T(8,128)(2,1)S(1)} %broadcast_in_dim.55), channel_id=1, replica_groups=mesh['zh'=4,'zl'=2,'y'=4,'x'=4,'c'=2] {'zl','y','x','c'}, dimensions={0} | all-to-all | bytes 262144 | tf_op jit(solution)/shard_map/all_to_all | solution.py:23
  172.8 4.7 %shard_map.74 = (bf16[4,48,1152]{2,1,0:T(8,128)(2,1)}, f32[48,1024]{1,0:T(8,128)}, f32[48,1024]{1,0:T(8,128)}, f32[48,256]{1,0:T(8,128)}, f32[48,128]{1,0:T(8,128)}) custom-call(bf16[512,128]{1,0:T(8,128)(2,1)} %bitcast.48, bf16[3072,128]{1,0:T(8,128)(2,1)} %bitcast.44, bf16[8,136,1024]{2,1,0:T(8,128)(2,1)} %copy-done, bf16[1024,256]{1,0:T(8,128)(2,1)} %bitcast.40, ...), custom_call_target="tpu_custom_call" | custom-call | tf_op jit(solution)/shard_map/pallas_call | solution.py:273
  177.5 18.0 %all_to_all.58.arrived = bf16[4,48,1152]{2,1,0:T(8,128)(2,1)} all-to-all(bf16[4,48,1152]{2,1,0:T(8,128)(2,1)} %get-tuple-element.33), channel_id=1, replica_groups=mesh['zh'=4,'zl'=2,'y'=4,'x'=4,'c'=2] {'zh'}, dimensions={0} | all-to-all | bytes 884736 | tf_op jit(solution)/shard_map/all_to_all | solution.py:23
  195.5 3.9 %shard_map.75 = (bf16[512,128]{1,0:T(8,128)(2,1)}, f32[48,1024]{1,0:T(8,128)}, f32[48,1024]{1,0:T(8,128)}) custom-call(bf16[4,48,1152]{2,1,0:T(8,128)(2,1)} %all_to_all.58.arrived, f32[48,1024]{1,0:T(8,128)} %get-tuple-element.34.direction_in.refs_6_, f32[48,1024]{1,0:T(8,128)} %get-tuple-element.30.refs_5_.residual_in, ...), custom_call_target="tpu_custom_call" | custom-call | tf_op jit(solution)/shard_map/pallas_call | solution.py:292
  199.4 14.5 %all_to_all.59 = bf16[64,8,128]{2,1,0:T(8,128)(2,1)S(1)} all-to-all(bf16[64,8,128]{2,1,0:T(8,128)(2,1)} %bitcast.52), channel_id=1, replica_groups=mesh['zh'=4,'zl'=2,'y'=4,'x'=4,'c'=2] {'zl','y','x','c'}, dimensions={0} | all-to-all | bytes 262144 | tf_op jit(solution)/shard_map/all_to_all | solution.py:23
  213.9 0.1 convert_reduce_fusion.2
  214.1 12.9 %all_to_all.60 = bf16[64,8,128]{2,1,0:T(8,128)(2,1)} all-to-all(bf16[64,8,128]{2,1,0:T(8,128)(2,1)S(1)} %broadcast_in_dim.56), channel_id=1, replica_groups=mesh['zh'=4,'zl'=2,'y'=4,'x'=4,'c'=2] {'zl','y','x','c'}, dimensions={0} | all-to-all | bytes 262144 | tf_op jit(solution)/shard_map/all_to_all | solution.py:23
  227.0 4.6 %shard_map.76 = (bf16[4,48,640]{2,1,0:T(8,128)(2,1)}, f32[48,1024]{1,0:T(8,128)}, f32[48,1024]{1,0:T(8,128)}, f32[48,256]{1,0:T(8,128)}, f32[48,128]{1,0:T(8,128)}) custom-call(bf16[512,128]{1,0:T(8,128)(2,1)} %bitcast.47, bf16[3072,128]{1,0:T(8,128)(2,1)} %bitcast.45, bf16[8,136,1024]{2,1,0:T(8,128)(2,1)} %copy-done, bf16[1024,256]{1,0:T(8,128)(2,1)} %bitcast.42, ...), custom_call_target="tpu_custom_call" | custom-call | tf_op jit(solution)/shard_map/pallas_call | solution.py:273
  231.6 3.4 %all-to-all-start.10 = ((bf16[4,48,640]{2,1,0:T(8,128)(2,1)}), bf16[4,48,640]{2,1,0:T(8,128)(2,1)S(1)}, u32[]{:S(2)}, u32[]{:S(2)}) async-start(bf16[4,48,640]{2,1,0:T(8,128)(2,1)} %get-tuple-element.43), calls=%async_computation.10 | async-start | bytes 491520 | tf_op jit(solution)/shard_map/all_to_all | solution.py:23
  235.0 1.0 slice_reduce_fusion
  236.0 7.8 %all-to-all-done.10 = bf16[4,48,640]{2,1,0:T(8,128)(2,1)S(1)} async-done(((bf16[4,48,640]{2,1,0:T(8,128)(2,1)}), bf16[4,48,640]{2,1,0:T(8,128)(2,1)S(1)}, u32[]{:S(2)}, u32[]{:S(2)}) %all-to-all-start.10) | async-done | bytes 245792 | tf_op jit(solution)/shard_map/all_to_all | solution.py:23
  243.8 0.2 fusion.4
  244.0 1.6 fusion.3
  (45 shorter events, 0.5 us)
Async XLA Ops:
  6.4 6.5 %copy-start.2 = (f32[256,256]{1,0:T(8,128)S(1)}, f32[256,256]{1,0:T(8,128)}, u32[]{:S(2)}) copy-start(f32[256,256]{1,0:T(8,128)} %param.7) | copy-start | bytes 786436
  6.4 34.8 %all-to-all-start = ((bf16[8,136,1024]{2,1,0:T(8,128)(2,1)}), bf16[8,136,1024]{2,1,0:T(8,128)(2,1)S(1)}, u32[]{:S(2)}, u32[]{:S(2)}) async-start(bf16[8,136,1024]{2,1,0:T(8,128)(2,1)} %shard_map.68), calls=%async_computation | async-start | bytes 4456448 | tf_op jit(solution)/shard_map/all_to_all | solution.py:23
  12.9 40.7 %collective-permute-start.1 = (bf16[256,256]{1,0:T(8,128)(2,1)S(1)}, bf16[256,256]{1,0:T(8,128)(2,1)}, u32[]{:S(2)}, u32[]{:S(2)}) collective-permute-start(bf16[256,256]{1,0:T(8,128)(2,1)S(1)} %convert_element_type.34), channel_id=1, source_target_pairs={{0,128},{64,192},{128,0},{192,64},{1,129},{65,193},{129,1},{193,65... | collective-permute-start | bytes 393224 | tf_op jit(solution)/shard_map/ppermute | solution.py:236
  19.0 35.6 %collective-permute-start = (bf16[256,256]{1,0:T(8,128)(2,1)S(1)}, bf16[256,256]{1,0:T(8,128)(2,1)S(1)}, u32[]{:S(2)}, u32[]{:S(2)}) collective-permute-start(bf16[256,256]{1,0:T(8,128)(2,1)S(1)} %convert_element_type.34), channel_id=1, source_target_pairs={{0,64},{64,128},{128,192},{192,0},{1,65},{65,129},{129,193},{193,1... | collective-permute-start | bytes 393224 | tf_op jit(solution)/shard_map/ppermute | solution.py:236
  20.2 34.6 %collective-permute-start.2 = (bf16[256,256]{1,0:T(8,128)(2,1)S(1)}, bf16[256,256]{1,0:T(8,128)(2,1)S(1)}, u32[]{:S(2)}, u32[]{:S(2)}) collective-permute-start(bf16[256,256]{1,0:T(8,128)(2,1)S(1)} %convert_element_type.34), channel_id=1, source_target_pairs={{0,192},{64,0},{128,64},{192,128},{1,193},{65,1},{129,65},{193,129... | collective-permute-start | bytes 393224 | tf_op jit(solution)/shard_map/ppermute | solution.py:236
  41.2 1.4 copy-start
  45.4 17.9 %all-to-all-start.1 = ((bf16[4,48,1280]{2,1,0:T(8,128)(2,1)}), bf16[4,48,1280]{2,1,0:T(8,128)(2,1)S(1)}, u32[]{:S(2)}, u32[]{:S(2)}) async-start(bf16[4,48,1280]{2,1,0:T(8,128)(2,1)} %shard_map.69), calls=%async_computation.1 | async-start | bytes 983040 | tf_op jit(solution)/shard_map/all_to_all | solution.py:23
  63.3 0.8 copy-start.1
  68.0 49.0 %copy-start.5 = (f32[256]{0:T(256)S(1)}, f32[256]{0:T(256)}, u32[]{:S(2)}) copy-start(f32[256]{0:T(256)} %param.8) | copy-start | bytes 3076
  68.0 29.1 %all-to-all-start.2 = ((bf16[64,48,128]{2,1,0:T(8,128)(2,1)}), bf16[64,48,128]{2,1,0:T(8,128)(2,1)S(1)}, u32[]{:S(2)}, u32[]{:S(2)}) async-start(bf16[64,48,128]{2,1,0:T(8,128)(2,1)} %bitcast.46), calls=%async_computation.2 | async-start | bytes 1572864 | tf_op jit(solution)/shard_map/all_to_all | solution.py:23
  117.6 23.5 %copy-start.4 = (f32[48]{0:T(128)S(1)}, f32[48]{0:T(128)}, u32[]{:S(2)}) copy-start(f32[48]{0:T(128)} %param.9) | copy-start | bytes 580
  145.5 14.3 %all-to-all-start.5 = ((bf16[64,8,128]{2,1,0:T(8,128)(2,1)}), bf16[64,8,128]{2,1,0:T(8,128)(2,1)S(1)}, u32[]{:S(2)}, u32[]{:S(2)}) async-start(bf16[64,8,128]{2,1,0:T(8,128)(2,1)} %bitcast.51), calls=%async_computation.5 | async-start | bytes 262144 | tf_op jit(solution)/shard_map/all_to_all | solution.py:23
  227.0 17.0 %copy-start.3 = (f32[48,256]{1,0:T(8,128)S(1)}, f32[48,256]{1,0:T(8,128)}, u32[]{:S(2)}) copy-start(f32[48,256]{1,0:T(8,128)} %get-tuple-element.45) | copy-start | bytes 147460
  231.6 12.2 %all-to-all-start.10 = ((bf16[4,48,640]{2,1,0:T(8,128)(2,1)}), bf16[4,48,640]{2,1,0:T(8,128)(2,1)S(1)}, u32[]{:S(2)}, u32[]{:S(2)}) async-start(bf16[4,48,640]{2,1,0:T(8,128)(2,1)} %get-tuple-element.43), calls=%async_computation.10 | async-start | bytes 491520 | tf_op jit(solution)/shard_map/all_to_all | solution.py:23

commit v3 on v2

--- a/solution.py
+++ b/solution.py
@@ -40,8 +40,11 @@
     return lax.dot_general(a, b, (((1,), (1,)), ((), ())), preferred_element_type=F32)
 
 
-def call(body, out, **kw):
-    return pl.pallas_call(body, out_shape=out, **kw)
+PARAMS = pltpu.CompilerParams(vmem_limit_bytes=20 * 1024 * 1024)
+
+
+def call(body, out):
+    return pl.pallas_call(body, out_shape=out, compiler_params=PARAMS)
 
 
 def shape(*dims, dtype=F32):
@@ -65,25 +68,14 @@
     return jnp.sum(array, axis=1, keepdims=True)
 
 
-def pack_kernel(a0, a1, a2, a3, goal, out):
-    for index, block in enumerate((a0, a1, a2, a3)):
-        out[0, :128, index * 256 : (index + 1) * 256] = block[...]
-    for index in range(6):
-        out[0, 128:136, index * 128 : (index + 1) * 128] = goal[index * 8 : index * 8 + 8, :]
-    out[0, 128:136, 768:] = jnp.zeros((8, 256), BF)
-
-
-def pack(design, goal):
-    def part(index):
-        return pl.BlockSpec((128, 256), lambda s, index=index: (0, index * 8 + s))
-
-    return pl.pallas_call(
-        pack_kernel,
-        grid=(8,),
-        in_specs=[part(0), part(1), part(2), part(3), pl.BlockSpec((T, 128), lambda s: (0, 0))],
-        out_specs=pl.BlockSpec((1, 136, BLOCK), lambda s: (s, 0, 0)),
-        out_shape=shape(8, 136, BLOCK, dtype=BF),
-    )(design, design, design, design, goal)
+def pack_kernel(design, goal, out):
+    for to in range(8):
+        for index in range(4):
+            at = (index * 8 + to) * 256
+            out[to, :128, index * 256 : (index + 1) * 256] = design[:, at : at + 256]
+        for index in range(6):
+            out[to, 128:136, index * 128 : (index + 1) * 128] = goal[index * 8 : index * 8 + 8, :]
+        out[to, 128:136, 768:] = jnp.zeros((8, 256), BF)
 
 
 def start_kernel(mat, out):
@@ -237,7 +229,7 @@
         slots = lax.dynamic_update_slice(slots, other[None], ((zh - shift) % N_ZH, 0, 0))
     fac = slots.reshape(BLOCK, RANK)
 
-    mat = exchange(pack(design, targets.T), OWN)
+    mat = exchange(call(pack_kernel, shape(8, 136, BLOCK, dtype=BF))(design, targets.T), OWN)
     arrived = call(start_kernel, shape(N_ZH, T, BLOCK + 256, dtype=BF))(mat)
     arrived = exchange(arrived, "zh")
     gram = lax.dot_general(fac, fac, (((0,), (0,)), ((), ())), preferred_element_type=F32)

time: 247 us -> 248 us (level)
  Pallas kernels: 37.4 us -> 12.1 us
  local copies, waits for them, and re-layouts: 7.18 us -> 29.9 us
  other arithmetic: 2.2 us -> 6.49 us
  blocking collectives: 96.6 us -> 93.5 us
  waiting for transfers between devices: 52.5 us -> 55.3 us
    unnamed x12 -> x82, local copies, waits for them, and re-layouts: 2.2 us -> 22 us
    pallas_call x3, Pallas kernels: 14 us -> 5.82 us  [shards(): call(lambda *refs, first=first, last=last: search_kernel(first, last, *re...]
    pallas_call x1, Pallas kernels: 5.76 us -> 0.21 us  [shards(): call(pack_kernel, shape(8, 136, BLOCK, dtype=BF))(design, targets.T)]
    all_to_all x6, blocking collectives: 96.6 us -> 93.5 us  [exchange(): return lax.all_to_all(pieces, axes, 0, 0, tiled=True)]
    pallas_call x1, Pallas kernels: 3.86 us -> 1.07 us  [shards(): call(next_kernel, (shape(HEAD, 128, dtype=BF), shape(T, BLOCK), shape(T,...]
    pallas_call x1, Pallas kernels: 3.75 us -> 1.06 us  [shards(): call(lambda a, d, r, s, p, m, f, *outs: next_kernel(a, d, r, None, s, p,...]
    pallas_call x1, Pallas kernels: 3.38 us -> 0.72 us  [shards(): rest = call(cross_kernel, shape(2560, 128, dtype=BF))(mat, fac, gram)]
  transfers between devices with their start and end apart: 8 -> 8, of which waited for: 5 -> 6; matrix products, arithmetic and copies ran while one was open for 2% -> 2% of each run, Pallas kernels for 3% -> 1%
where the time goes in v3:
time: 248 us; the launch traced here: 247 us
  blocking collectives  93.5 us (38%)
  waiting for transfers between devices  55.3 us (22%)
  starting transfers between devices  47.7 us (19%)
  local copies, waits for them, and re-layouts  29.9 us (12%)
  Pallas kernels  12.1 us (5%)
  other arithmetic  6.49 us (3%)
    all_to_all x6, blocking collectives, exchange(): return lax.all_to_all(pieces, axes, 0, 0, tiled=True)  93.5 us
    all_to_all x5, waiting for transfers between devices, exchange(): return lax.all_to_all(pieces, axes, 0, 0, tiled=True)  53.5 us
    all_to_all x5, starting transfers between devices, exchange(): return lax.all_to_all(pieces, axes, 0, 0, tiled=True)  38.1 us
    unnamed x82, local copies, waits for them, and re-layouts  22 us
    ppermute x3, starting transfers between devices, shards(): other = lax.ppermute(low_factor, 'zh', pairs)  9.67 us
    pallas_call x3, Pallas kernels, shards(): call(lambda *refs, first=first, last=last: search_kernel(first, last, *re...  5.82 us
  transfers between devices with their start and end apart: 8, of which 6 were waited for; matrix products, arithmetic and copies ran while one was open for 2% of the time, Pallas kernels for 1%

profile of v3, /device:TPU:1, one launch (start us, length us, event | category | flops | bytes accessed | tf_op | source)
XLA Modules:
  0.0 246.5 jit_solution(16682065648709210628)
XLA Ops:
  0.6 1.6 copy-done.1
  3.2 1.4 copy-done
  4.5 6.5 %all-to-all-start = ((bf16[8,136,1024]{2,1,0:T(8,128)(2,1)}), bf16[8,136,1024]{2,1,0:T(8,128)(2,1)S(1)}, u32[]{:S(2)}, u32[]{:S(2)}) async-start(bf16[8,136,1024]{2,1,0:T(8,128)(2,1)} %copy-done), calls=%async_computation | async-start | bytes 4456448 | tf_op jit(solution)/shard_map/all_to_all | solution.py:23
  11.0 6.1 %collective-permute-start.1 = (bf16[256,256]{1,0:T(8,128)(2,1)S(1)}, bf16[256,256]{1,0:T(8,128)(2,1)}, u32[]{:S(2)}, u32[]{:S(2)}) collective-permute-start(bf16[256,256]{1,0:T(8,128)(2,1)S(1)} %convert_element_type.34), channel_id=1, source_target_pairs={{0,128},{64,192},{128,0},{192,64},{1,129},{65,193},{129,1},{193,65... | collective-permute-start | bytes 393224 | tf_op jit(solution)/shard_map/ppermute | solution.py:228
  17.1 1.2 collective-permute-start
  18.3 2.4 collective-permute-start.2
  20.7 18.6 %all-to-all-done.mat.refs_1_.m.refs_2_ = bf16[8,136,1024]{2,1,0:T(8,128)(2,1)S(1)} async-done(((bf16[8,136,1024]{2,1,0:T(8,128)(2,1)}), bf16[8,136,1024]{2,1,0:T(8,128)(2,1)S(1)}, u32[]{:S(2)}, u32[]{:S(2)}) %all-to-all-start) | async-done | bytes 2228256 | tf_op jit(solution)/shard_map/all_to_all | solution.py:23
  39.3 1.2 shard_map.69
  40.6 7.9 %all-to-all-start.1 = ((bf16[4,48,1280]{2,1,0:T(8,128)(2,1)}), bf16[4,48,1280]{2,1,0:T(8,128)(2,1)}, u32[]{:S(2)}, u32[]{:S(2)}) async-start(bf16[4,48,1280]{2,1,0:T(8,128)(2,1)} %shard_map.69), calls=%async_computation.1 | async-start | bytes 983040 | tf_op jit(solution)/shard_map/all_to_all | solution.py:23
  48.8 1.0 copy.17
  49.8 1.8 collective-permute-done
  51.6 1.0 copy.16
  53.4 0.7 shard_map.70.rest
  54.1 3.9 %all-to-all-done.1.arrived = bf16[4,48,1280]{2,1,0:T(8,128)(2,1)} async-done(((bf16[4,48,1280]{2,1,0:T(8,128)(2,1)}), bf16[4,48,1280]{2,1,0:T(8,128)(2,1)}, u32[]{:S(2)}, u32[]{:S(2)}) %all-to-all-start.1) | async-done | bytes 491552 | tf_op jit(solution)/shard_map/all_to_all | solution.py:23
  58.0 2.0 shard_map.71
  60.7 0.9 copy-done.11
  62.2 13.7 %all-to-all-start.2 = ((bf16[64,48,128]{2,1,0:T(8,128)(2,1)}), bf16[64,48,128]{2,1,0:T(8,128)(2,1)S(1)}, u32[]{:S(2)}, u32[]{:S(2)}) async-start(bf16[64,48,128]{2,1,0:T(8,128)(2,1)} %bitcast.46), calls=%async_computation.2 | async-start | bytes 1572864 | tf_op jit(solution)/shard_map/all_to_all | solution.py:23
  75.9 14.7 %all-to-all-done.2 = bf16[64,48,128]{2,1,0:T(8,128)(2,1)S(1)} async-done(((bf16[64,48,128]{2,1,0:T(8,128)(2,1)}), bf16[64,48,128]{2,1,0:T(8,128)(2,1)S(1)}, u32[]{:S(2)}, u32[]{:S(2)}) %all-to-all-start.2) | async-done | bytes 786464 | tf_op jit(solution)/shard_map/all_to_all | solution.py:23
  91.4 0.7 slice.96
  93.0 19.4 %all_to_all.55 = bf16[64,48,128]{2,1,0:T(8,128)(2,1)S(1)} all-to-all(bf16[64,48,128]{2,1,0:T(8,128)(2,1)S(1)} %broadcast_in_dim.25), channel_id=1, replica_groups=mesh['zh'=4,'zl'=2,'y'=4,'x'=4,'c'=2] {'zl','y','x','c'}, dimensions={0} | all-to-all | bytes 1572864 | tf_op jit(solution)/shard_map/all_to_all | solution.py:23
  112.4 0.9 copy-done.3
  113.3 1.9 shard_map.72
  115.9 18.5 %all_to_all.56.a = bf16[4,48,1152]{2,1,0:T(8,128)(2,1)S(1)} all-to-all(bf16[4,48,1152]{2,1,0:T(8,128)(2,1)S(1)} %get-tuple-element.26), channel_id=1, replica_groups=mesh['zh'=4,'zl'=2,'y'=4,'x'=4,'c'=2] {'zh'}, dimensions={0} | all-to-all | bytes 884736 | tf_op jit(solution)/shard_map/all_to_all | solution.py:23
  134.5 1.1 shard_map.73
  137.6 6.5 %all-to-all-start.5 = ((bf16[64,8,128]{2,1,0:T(8,128)(2,1)}), bf16[64,8,128]{2,1,0:T(8,128)(2,1)}, u32[]{:S(2)}, u32[]{:S(2)}) async-start(bf16[64,8,128]{2,1,0:T(8,128)(2,1)} %bitcast.49), calls=%async_computation.5 | async-start | bytes 262144 | tf_op jit(solution)/shard_map/all_to_all | solution.py:23
  144.1 8.5 %all-to-all-done.5 = bf16[64,8,128]{2,1,0:T(8,128)(2,1)} async-done(((bf16[64,8,128]{2,1,0:T(8,128)(2,1)}), bf16[64,8,128]{2,1,0:T(8,128)(2,1)}, u32[]{:S(2)}, u32[]{:S(2)}) %all-to-all-start.5) | async-done | bytes 131104 | tf_op jit(solution)/shard_map/all_to_all | solution.py:23
  152.6 1.0 convert_reduce_fusion.3
  156.7 12.6 %all_to_all.57 = bf16[64,8,128]{2,1,0:T(8,128)(2,1)S(1)} all-to-all(bf16[64,8,128]{2,1,0:T(8,128)(2,1)S(1)} %broadcast_in_dim.55), channel_id=1, replica_groups=mesh['zh'=4,'zl'=2,'y'=4,'x'=4,'c'=2] {'zl','y','x','c'}, dimensions={0} | all-to-all | bytes 262144 | tf_op jit(solution)/shard_map/all_to_all | solution.py:23
  169.3 0.9 copy-done.5
  170.2 0.9 copy-done.7
  171.2 0.9 copy-done.20
  172.1 0.7 copy-done.27
  172.8 0.8 copy-done.32
  173.6 1.7 shard_map.74
  176.0 16.2 %all_to_all.58.arrived = bf16[4,48,1152]{2,1,0:T(8,128)(2,1)S(1)} all-to-all(bf16[4,48,1152]{2,1,0:T(8,128)(2,1)S(1)} %get-tuple-element.33), channel_id=1, replica_groups=mesh['zh'=4,'zl'=2,'y'=4,'x'=4,'c'=2] {'zh'}, dimensions={0} | all-to-all | bytes 884736 | tf_op jit(solution)/shard_map/all_to_all | solution.py:23
  192.2 1.1 shard_map.75
  193.9 14.2 %all_to_all.59 = bf16[64,8,128]{2,1,0:T(8,128)(2,1)S(1)} all-to-all(bf16[64,8,128]{2,1,0:T(8,128)(2,1)S(1)} %bitcast.50), channel_id=1, replica_groups=mesh['zh'=4,'zl'=2,'y'=4,'x'=4,'c'=2] {'zl','y','x','c'}, dimensions={0} | all-to-all | bytes 262144 | tf_op jit(solution)/shard_map/all_to_all | solution.py:23
  211.3 12.6 %all_to_all.60 = bf16[64,8,128]{2,1,0:T(8,128)(2,1)S(1)} all-to-all(bf16[64,8,128]{2,1,0:T(8,128)(2,1)S(1)} %broadcast_in_dim.56), channel_id=1, replica_groups=mesh['zh'=4,'zl'=2,'y'=4,'x'=4,'c'=2] {'zl','y','x','c'}, dimensions={0} | all-to-all | bytes 262144 | tf_op jit(solution)/shard_map/all_to_all | solution.py:23
  224.0 0.9 copy-done.10
  224.9 0.9 copy-done.13
  225.8 0.9 copy-done.18
  226.8 0.7 copy-done.25
  227.5 0.8 copy-done.30
  228.3 2.2 shard_map.76
  232.5 3.4 %all-to-all-start.10 = ((bf16[4,48,640]{2,1,0:T(8,128)(2,1)}), bf16[4,48,640]{2,1,0:T(8,128)(2,1)S(1)}, u32[]{:S(2)}, u32[]{:S(2)}) async-start(bf16[4,48,640]{2,1,0:T(8,128)(2,1)} %copy-done.14), calls=%async_computation.10 | async-start | bytes 491520 | tf_op jit(solution)/shard_map/all_to_all | solution.py:23
  235.9 1.0 slice_reduce_fusion
  236.9 7.8 %all-to-all-done.10 = bf16[4,48,640]{2,1,0:T(8,128)(2,1)S(1)} async-done(((bf16[4,48,640]{2,1,0:T(8,128)(2,1)}), bf16[4,48,640]{2,1,0:T(8,128)(2,1)S(1)}, u32[]{:S(2)}, u32[]{:S(2)}) %all-to-all-start.10) | async-done | bytes 245792 | tf_op jit(solution)/shard_map/all_to_all | solution.py:23
  244.9 1.6 fusion.3
  (115 shorter events, 17.3 us)
Async XLA Ops:
  0.6 1.6 copy-start.1
  2.2 0.7 copy-start.34
  3.1 1.4 copy-start
  4.5 6.5 %copy-start.37 = (f32[256,256]{1,0:T(8,128)S(1)}, f32[256,256]{1,0:T(8,128)}, u32[]{:S(2)}) copy-start(f32[256,256]{1,0:T(8,128)} %param.7) | copy-start | bytes 786436
  4.5 34.8 %all-to-all-start = ((bf16[8,136,1024]{2,1,0:T(8,128)(2,1)}), bf16[8,136,1024]{2,1,0:T(8,128)(2,1)S(1)}, u32[]{:S(2)}, u32[]{:S(2)}) async-start(bf16[8,136,1024]{2,1,0:T(8,128)(2,1)} %copy-done), calls=%async_computation | async-start | bytes 4456448 | tf_op jit(solution)/shard_map/all_to_all | solution.py:23
  11.0 37.7 %collective-permute-start.1 = (bf16[256,256]{1,0:T(8,128)(2,1)S(1)}, bf16[256,256]{1,0:T(8,128)(2,1)}, u32[]{:S(2)}, u32[]{:S(2)}) collective-permute-start(bf16[256,256]{1,0:T(8,128)(2,1)S(1)} %convert_element_type.34), channel_id=1, source_target_pairs={{0,128},{64,192},{128,0},{192,64},{1,129},{65,193},{129,1},{193,65... | collective-permute-start | bytes 393224 | tf_op jit(solution)/shard_map/ppermute | solution.py:228
  17.1 34.5 %collective-permute-start = (bf16[256,256]{1,0:T(8,128)(2,1)S(1)}, bf16[256,256]{1,0:T(8,128)(2,1)}, u32[]{:S(2)}, u32[]{:S(2)}) collective-permute-start(bf16[256,256]{1,0:T(8,128)(2,1)S(1)} %convert_element_type.34), channel_id=1, source_target_pairs={{0,64},{64,128},{128,192},{192,0},{1,65},{65,129},{129,193},{193,1... | collective-permute-start | bytes 393224 | tf_op jit(solution)/shard_map/ppermute | solution.py:228
  18.3 34.3 %collective-permute-start.2 = (bf16[256,256]{1,0:T(8,128)(2,1)S(1)}, bf16[256,256]{1,0:T(8,128)(2,1)S(1)}, u32[]{:S(2)}, u32[]{:S(2)}) collective-permute-start(bf16[256,256]{1,0:T(8,128)(2,1)S(1)} %convert_element_type.34), channel_id=1, source_target_pairs={{0,192},{64,0},{128,64},{192,128},{1,193},{65,1},{129,65},{193,129... | collective-permute-start | bytes 393224 | tf_op jit(solution)/shard_map/ppermute | solution.py:228
  40.6 17.5 %all-to-all-start.1 = ((bf16[4,48,1280]{2,1,0:T(8,128)(2,1)}), bf16[4,48,1280]{2,1,0:T(8,128)(2,1)}, u32[]{:S(2)}, u32[]{:S(2)}) async-start(bf16[4,48,1280]{2,1,0:T(8,128)(2,1)} %shard_map.69), calls=%async_computation.1 | async-start | bytes 983040 | tf_op jit(solution)/shard_map/all_to_all | solution.py:23
  60.0 0.7 copy-start.2
  60.7 0.9 copy-start.11
  61.6 0.6 copy-start.33
  62.2 50.2 %copy-start.40 = (f32[256]{0:T(256)S(1)}, f32[256]{0:T(256)}, u32[]{:S(2)}) copy-start(f32[256]{0:T(256)} %param.8) | copy-start | bytes 3076
  62.2 28.4 %all-to-all-start.2 = ((bf16[64,48,128]{2,1,0:T(8,128)(2,1)}), bf16[64,48,128]{2,1,0:T(8,128)(2,1)S(1)}, u32[]{:S(2)}, u32[]{:S(2)}) async-start(bf16[64,48,128]{2,1,0:T(8,128)(2,1)} %bitcast.46), calls=%async_computation.2 | async-start | bytes 1572864 | tf_op jit(solution)/shard_map/all_to_all | solution.py:23
  90.7 0.6 copy-start.38
  112.4 0.9 copy-start.3
  113.3 21.1 %copy-start.39 = (f32[48]{0:T(128)S(1)}, f32[48]{0:T(128)}, u32[]{:S(2)}) copy-start(f32[48]{0:T(128)} %param.9) | copy-start | bytes 580
  115.2 0.7 copy-start.19
  115.9 18.6 %copy-start.31 = (f32[48,256]{1,0:T(8,128)}, f32[48,256]{1,0:T(8,128)S(1)}, u32[]{:S(2)}) copy-start(f32[48,256]{1,0:T(8,128)S(1)} %get-tuple-element.32.refs_8_) | copy-start | bytes 147460
  115.9 19.6 %copy-start.4 = (f32[48,1024]{1,0:T(8,128)}, f32[48,1024]{1,0:T(8,128)S(1)}, u32[]{:S(2)}) copy-start(f32[48,1024]{1,0:T(8,128)S(1)} %get-tuple-element.27.d.refs_6_) | copy-start | bytes 589828
  115.9 19.6 %copy-start.26 = (f32[48,128]{1,0:T(8,128)}, f32[48,128]{1,0:T(8,128)S(1)}, u32[]{:S(2)}) copy-start(f32[48,128]{1,0:T(8,128)S(1)} %get-tuple-element.28.s.refs_9_) | copy-start | bytes 73732
  134.5 3.1 %copy-start.15 = (f32[48,128]{1,0:T(8,128)}, f32[48,128]{1,0:T(8,128)S(1)}, u32[]{:S(2)}) copy-start(f32[48,128]{1,0:T(8,128)S(1)} %broadcast_in_dim.54.p.penalty) | copy-start | bytes 73732
  135.5 0.7 copy-start.6
  136.2 0.7 copy-start.21
  136.9 0.7 copy-start.23
  137.6 15.1 %all-to-all-start.5 = ((bf16[64,8,128]{2,1,0:T(8,128)(2,1)}), bf16[64,8,128]{2,1,0:T(8,128)(2,1)}, u32[]{:S(2)}, u32[]{:S(2)}) async-start(bf16[64,8,128]{2,1,0:T(8,128)(2,1)} %bitcast.49), calls=%async_computation.5 | async-start | bytes 262144 | tf_op jit(solution)/shard_map/all_to_all | solution.py:23
  169.3 0.9 copy-start.5
  170.2 0.9 copy-start.7
  171.2 0.9 copy-start.20
  172.1 0.7 copy-start.27
  172.8 0.8 copy-start.32
  173.6 18.5 %copy-start.8 = (f32[48,1024]{1,0:T(8,128)S(1)}, f32[48,1024]{1,0:T(8,128)}, u32[]{:S(2)}) copy-start(f32[48,1024]{1,0:T(8,128)} %copy-done.6) | copy-start | bytes 589828
  173.6 18.5 %copy-start.16 = (f32[48,128]{1,0:T(8,128)S(1)}, f32[48,128]{1,0:T(8,128)}, u32[]{:S(2)}) copy-start(f32[48,128]{1,0:T(8,128)} %copy-done.15) | copy-start | bytes 73732
  173.6 18.5 %copy-start.22 = (f32[48,1024]{1,0:T(8,128)S(1)}, f32[48,1024]{1,0:T(8,128)}, u32[]{:S(2)}) copy-start(f32[48,1024]{1,0:T(8,128)} %copy-done.21) | copy-start | bytes 589828
  175.3 0.6 copy-start.29
  176.0 16.2 %copy-start.17 = (f32[48,1024]{1,0:T(8,128)}, f32[48,1024]{1,0:T(8,128)S(1)}, u32[]{:S(2)}) copy-start(f32[48,1024]{1,0:T(8,128)S(1)} %get-tuple-element.40.refs_7_) | copy-start | bytes 589828
  176.0 17.3 %copy-start.9 = (f32[48,1024]{1,0:T(8,128)}, f32[48,1024]{1,0:T(8,128)S(1)}, u32[]{:S(2)}) copy-start(f32[48,1024]{1,0:T(8,128)S(1)} %get-tuple-element.34.direction_in.refs_6_) | copy-start | bytes 589828
  176.0 17.3 %copy-start.24 = (f32[48,128]{1,0:T(8,128)}, f32[48,128]{1,0:T(8,128)S(1)}, u32[]{:S(2)}) copy-start(f32[48,128]{1,0:T(8,128)S(1)} %get-tuple-element.36.scal_in.refs_9_) | copy-start | bytes 73732
  193.3 0.7 copy-start.12
  193.9 14.2 %copy-start.35 = (f32[48,1024]{1,0:T(8,128)}, f32[48,1024]{1,0:T(8,128)S(1)}, u32[]{:S(2)}) copy-start(f32[48,1024]{1,0:T(8,128)S(1)} %get-tuple-element.37) | copy-start | bytes 589828
  224.0 0.9 copy-start.10
  224.9 0.9 copy-start.13
  225.8 0.9 copy-start.18
  226.8 0.7 copy-start.25
  227.5 0.8 copy-start.30
  230.5 0.7 copy-start.14
  231.8 0.7 copy-start.36
  232.5 12.2 %all-to-all-start.10 = ((bf16[4,48,640]{2,1,0:T(8,128)(2,1)}), bf16[4,48,640]{2,1,0:T(8,128)(2,1)S(1)}, u32[]{:S(2)}, u32[]{:S(2)}) async-start(bf16[4,48,640]{2,1,0:T(8,128)(2,1)} %copy-done.14), calls=%async_computation.10 | async-start | bytes 491520 | tf_op jit(solution)/shard_map/all_to_all | solution.py:23
  (1 other events, 0.6 us)

commit v4 on v3

v4 whole, which is shorter than its diff:
```python
import jax
import jax.numpy as jnp
from jax import lax
from jax.experimental import pallas as pl
from jax.experimental.pallas import tpu as pltpu
from jax.sharding import Mesh
from jax.sharding import PartitionSpec as P

ITERS = 3
ROW = ("zh", "zl", "y")
FEAT = ("x", "c")
OWN = ("zl", "y")
MANY = ("zl", "y", "x", "c")
N_OWN, N_MANY, N_ZH = 8, 64, 4
T, RANK, BLOCK = 48, 256, 1024
SCAL = 480
HEAD = 512
BF = jnp.bfloat16
F32 = jnp.float32


def exchange(pieces, axes):
    return lax.all_to_all(pieces, axes, 0, 0, tiled=True)


def dot(a, b):
    return jnp.dot(a, b, preferred_element_type=F32)


def dot_t(a, b):
    return lax.dot_general(a, b, (((1,), (1,)), ((), ())), preferred_element_type=F32)


PARAMS = pltpu.CompilerParams(vmem_limit_bytes=20 * 1024 * 1024)


IN_HBM = pl.BlockSpec(memory_space=pltpu.HBM)
IN_VMEM = pl.BlockSpec(memory_space=pltpu.VMEM)
IN_SMEM = pl.BlockSpec(memory_space=pltpu.SMEM)


def call(body, out):
    return pl.pallas_call(body, out_shape=out, compiler_params=PARAMS)


def fetch(pairs, sems):
    copies = [pltpu.make_async_copy(a, b, sems.at[i]) for i, (a, b) in enumerate(pairs)]
    for copy in copies:
        copy.start()
    return copies


def shape(*dims, dtype=F32):
    return jax.ShapeDtypeStruct(dims, dtype)


def columns(parts):
    lane = lax.broadcasted_iota(jnp.int32, (T, 128), 1)
    block = jnp.zeros((T, 128), F32)
    for index, part in enumerate(parts):
        block = jnp.where(lane == index, part, block)
    return block


def split16(value):
    high = value.astype(BF).astype(F32)
    return high, value - high


def total_of(array):
    return jnp.sum(array, axis=1, keepdims=True)


def pack_kernel(design, goal, out, sems, goal_sems):
    copies = []
    for to in range(8):
        for index in range(4):
            at = (index * 8 + to) * 256
            copies.append(
                pltpu.make_async_copy(
                    design.at[:, at : at + 256],
                    out.at[to, :128, index * 256 : (index + 1) * 256],
                    sems.at[to * 4 + index],
                )
            )
        for index in range(6):
            copies.append(
                pltpu.make_async_copy(
                    goal.at[index * 8 : index * 8 + 8, :],
                    out.at[to, 128:136, index * 128 : (index + 1) * 128],
                    goal_sems.at[to * 6 + index],
                )
            )
    for copy in copies:
        copy.start()
    for copy in copies:
        copy.wait()


def pack(design, goal):
    return pl.pallas_call(
        pack_kernel,
        out_shape=shape(8, 136, BLOCK, dtype=BF),
        in_specs=[IN_HBM, IN_VMEM],
        out_specs=IN_HBM,
        scratch_shapes=[pltpu.SemaphoreType.DMA((32,)), pltpu.SemaphoreType.DMA((48,))],
    )(design, goal)


def start_kernel(mat, out):
    part = jnp.zeros((T, BLOCK), F32)
    for src in range(8):
        goal = jnp.concatenate(
            [mat[src, 128:136, t * 128 : (t + 1) * 128].astype(F32) for t in range(6)], axis=0
        ).astype(BF)
        part = part + dot(goal, mat[src, :128, :])
    high, low = split16(part)
    high, low = high.astype(BF), low.astype(BF)
    for to in range(N_ZH):
        out[to, :, :BLOCK] = high
        out[to, :, BLOCK:] = low[:, to * 256 : (to + 1) * 256]


def cross_kernel(mat, fac, gram, out):
    factor = fac[...]
    for src in range(8):
        block = dot(mat[src, :128, :], factor).astype(BF)
        out[src * 256 : src * 256 + 128, :] = block[:, :128]
        out[src * 256 + 128 : src * 256 + 256, :] = block[:, 128:]
    both = gram[...].astype(BF)
    out[2048:2304, :] = both[:, :128]
    out[2304:2560, :] = both[:, 128:]


def write_head(residual, direction, mat, fac, out):
    low = residual.astype(BF)
    for src in range(8):
        out[src * T : (src + 1) * T, :] = dot_t(low, mat[src, :128, :]).astype(BF)
    seen = dot(low, fac[...]).astype(BF)
    out[384:432, :] = seen[:, :128]
    out[432:480, :] = seen[:, 128:]
    rr = split16(total_of(residual * residual))
    rd = split16(total_of(residual * direction))
    block = jnp.concatenate([columns([*rr, *rd]), jnp.zeros((80, 128), F32)], axis=0)
    tile = block.T[:32, :]
    out[SCAL:HEAD, :] = tile.astype(BF)


def first_kernel(arrived, mat, fac, rest, out, start_out, held, sem):
    total = jnp.zeros((T, BLOCK + 256), F32)
    for source in range(N_ZH):
        total = total + arrived[source].astype(F32)
    held[...] = total
    store = pltpu.make_async_copy(held, start_out, sem.at[0])
    store.start()
    residual = total[:, :BLOCK]
    write_head(residual, residual, mat, fac, out)
    out[HEAD:, :] = rest[...]
    store.wait()


def first_call(arrived, mat, fac, rest):
    return pl.pallas_call(
        first_kernel,
        out_shape=(shape(3072, 128, dtype=BF), shape(T, BLOCK + 256)),
        in_specs=[IN_VMEM] * 4,
        out_specs=(IN_VMEM, IN_HBM),
        scratch_shapes=[pltpu.VMEM((T, BLOCK + 256), F32), pltpu.SemaphoreType.DMA((1,))],
        compiler_params=PARAMS,
    )(arrived, mat, fac, rest)


def own_part(array, zh):
    mine = array[:, :256]
    for index in range(1, N_ZH):
        mine = jnp.where(zh == index, array[:, index * 256 : (index + 1) * 256], mine)
    return mine


D_AT, R_AT, S_AT, C_AT, WIDE = 0, BLOCK, 2 * BLOCK, 2 * BLOCK + RANK, 2 * BLOCK + RANK + 128


def next_kernel(more, arrived, zh, penalty, mat, state, residual_in, fac_in, *refs):
    refs = list(refs)
    answer_in = refs.pop(0) if more else None
    out, residual_out, answer_out, direction_v, scal_v, residual_v, fac_v, answer_v, sems = refs
    copies = fetch(
        [
            (state.at[:, D_AT:R_AT], direction_v),
            (state.at[:, C_AT:WIDE], scal_v),
            (residual_in.at[:, :BLOCK], residual_v),
            (fac_in, fac_v),
        ]
        + ([(answer_in, answer_v)] if more else []),
        sems,
    )
    hess = jnp.zeros((T, BLOCK + 128), F32)
    for source in range(N_ZH):
        hess = hess + arrived[source].astype(F32)
    square = hess[:, BLOCK : BLOCK + 1] + hess[:, BLOCK + 1 : BLOCK + 2]
    hess = hess[:, :BLOCK]
    ridge = penalty[:, :1]
    for copy in copies[:3]:
        copy.wait()
    inner, dd = scal_v[:, :1], scal_v[:, 1:2]
    direction = direction_v[...]
    step = inner / (square + ridge * dd)
    residual = residual_v[...] - step * (hess + ridge * direction)
    residual_v[...] = residual
    answer = step * own_part(direction, zh[0])
    if more:
        copies[4].wait()
        answer = answer_v[...] + answer
    answer_v[...] = answer
    stores = [
        pltpu.make_async_copy(residual_v, residual_out, sems.at[5]),
        pltpu.make_async_copy(answer_v, answer_out, sems.at[6]),
    ]
    for copy in stores:
        copy.start()
    copies[3].wait()
    write_head(residual, direction, mat, fac_v, out)
    for copy in stores:
        copy.wait()


def next_call(arrived, zh, ridge, mat, state, residual, fac, answer):
    more = answer is not None
    extra = (answer,) if more else ()
    return pl.pallas_call(
        lambda *refs: next_kernel(more, *refs),
        out_shape=(shape(HEAD, 128, dtype=BF), shape(T, BLOCK), shape(T, 256)),
        in_specs=[IN_VMEM, IN_SMEM, IN_VMEM, IN_VMEM] + [IN_HBM] * (3 + len(extra)),
        out_specs=(IN_VMEM, IN_HBM, IN_HBM),
        scratch_shapes=[
            pltpu.VMEM((T, BLOCK), F32),
            pltpu.VMEM((T, 128), F32),
            pltpu.VMEM((T, BLOCK), F32),
            pltpu.VMEM((BLOCK, RANK), BF),
            pltpu.VMEM((T, 256), F32),
            pltpu.SemaphoreType.DMA((7,)),
        ],
        compiler_params=PARAMS,
    )(arrived, zh, ridge, mat, state, residual, fac, *extra)


def search_kernel(first, last, back, zh, weights, mat, residual_in, fac_in, *refs):
    refs = list(refs)
    state_in = None if first else refs.pop(0)
    full = back if first else refs.pop(0)
    answer_in, fix_in = (refs.pop(0), refs.pop(0)) if last else (None, None)
    out, state_out, residual_v, fac_v, sems = refs[:5]
    refs = refs[5:]
    pairs = [(residual_in.at[:, :BLOCK], residual_v), (fac_in, fac_v)]
    if not first:
        state_v, full_v = refs[:2]
        pairs += [(state_in, state_v), (full.at[HEAD:, :], full_v)]
        full, base = full_v, 0
    else:
        state_v = refs[0]
        base = HEAD
    if last:
        answer_v, fix_v, tail_v = refs[2:]
        pairs += [(answer_in, answer_v), (fix_in.at[:, BLOCK:], fix_v)]
    copies = fetch(pairs, sems)

    projected = jnp.concatenate([back[384:432, :], back[432:480, :]], axis=1).astype(F32)
    tile = jnp.concatenate([back[SCAL:HEAD, :].astype(F32), jnp.zeros((96, 128), F32)], axis=0).T
    rr = tile[:T, 0:1] + tile[:T, 1:2]
    rd = tile[:T, 2:3] + tile[:T, 3:4]
    scaled = weights[0:1, :] * projected
    cross_inner = total_of(scaled * projected)
    inner = rr + cross_inner
    low = scaled.astype(BF)
    if not first:
        copies[2].wait()
        copies[3].wait()
    gram = base + 2048
    through = jnp.concatenate(
        [dot(low, full[gram : gram + 256, :]), dot(low, full[gram + 256 : gram + 512, :])], axis=1
    )
    dd = rr + 2.0 * cross_inner + total_of(scaled * through)
    seen = projected + through
    if not first:
        before, dd_before = state_v[:, C_AT : C_AT + 1], state_v[:, C_AT + 1 : C_AT + 2]
        beta = inner / before
        sd = rd + total_of(scaled * state_v[:, S_AT:C_AT])
        dd = dd + 2.0 * beta * sd + beta * beta * dd_before
        seen = seen + beta * state_v[:, S_AT:C_AT]
    part = jnp.zeros((T, BLOCK), F32)
    square = jnp.zeros((T, 1), F32)
    for src in range(8):
        at = base + src * 256
        row = back[src * T : (src + 1) * T, :].astype(F32)
        row = row + dot_t(low[:, :128], full[at : at + 128, :])
        row = row + dot_t(low[:, 128:], full[at + 128 : at + 256, :])
        lanes = slice(R_AT + src * 128, R_AT + (src + 1) * 128)
        if not first:
            row = row + beta * state_v[:, lanes]
        state_v[:, lanes] = row
        row_low = row.astype(BF)
        square = square + total_of(row * row_low.astype(F32))
        part = part + dot(row_low, mat[src, :128, :])
    copies[0].wait()
    copies[1].wait()
    direction = residual_v[...] + dot_t(low, fac_v[...])
    if not first:
        direction = direction + beta * state_v[:, D_AT:R_AT]
    if last:
        copies[4].wait()
        copies[5].wait()
        tail_v[:, :256] = own_part(direction, zh[0])
        tail_v[:, 256:512] = answer_v[...]
        tail_v[:, 512:768] = own_part(residual_v[...], zh[0]) + fix_v[...]
        tail_v[:, 768:] = columns([inner, dd])
        store = pltpu.make_async_copy(tail_v, state_out, sems.at[6])
    else:
        state_v[:, D_AT:R_AT] = direction
        state_v[:, S_AT:C_AT] = seen
        state_v[:, C_AT:WIDE] = columns([inner, dd])
        store = pltpu.make_async_copy(state_v, state_out, sems.at[6])
    store.start()
    extra = columns(split16(square)).astype(BF)
    high, low = split16(part)
    high, low = high.astype(BF), low.astype(BF)
    for to in range(N_ZH):
        if last:
            mine = slice(to * 256, (to + 1) * 256)
            out[to, :, :256] = high[:, mine]
            out[to, :, 256:512] = low[:, mine]
            out[to, :, 512:] = extra
        else:
            out[to, :, :BLOCK] = high
            out[to, :, BLOCK:] = extra
    store.wait()


def search_call(first, last, back, zh, weights, mat, residual, fac, state, full, answer, fix):
    hbm = [residual, fac]
    if not first:
        hbm += [state, full]
    if last:
        hbm += [answer, fix]
    scratch = [
        pltpu.VMEM((T, BLOCK), F32),
        pltpu.VMEM((BLOCK, RANK), BF),
        pltpu.SemaphoreType.DMA((7,)),
        pltpu.VMEM((T, WIDE), F32),
    ]
    if not first:
        scratch.append(pltpu.VMEM((2560, 128), BF))
    if last:
        scratch += [pltpu.VMEM((T, 256), F32), pltpu.VMEM((T, 256), F32), pltpu.VMEM((T, 896), F32)]
    return pl.pallas_call(
        lambda *refs: search_kernel(first, last, *refs),
        out_shape=(
            shape(N_ZH, T, 640 if last else BLOCK + 128, dtype=BF),
            shape(T, 896 if last else WIDE),
        ),
        in_specs=[IN_VMEM, IN_SMEM, IN_VMEM, IN_VMEM] + [IN_HBM] * len(hbm),
        out_specs=(IN_VMEM, IN_HBM),
        scratch_shapes=scratch,
        compiler_params=PARAMS,
    )(back, zh, weights, mat, *hbm)


def middle_kernel(pieces, me, out):
    count = pieces.shape[1]
    total = jnp.zeros((count, 128), F32)
    for source in range(N_MANY):
        total = total + pieces[source].astype(F32)
    tile = total[:8]
    high_a, low_a = split16(tile[0:1] + tile[1:2])
    high_b, low_b = split16(tile[2:3] + tile[3:4])
    line = lax.broadcasted_iota(jnp.int32, (8, 128), 0)
    again = tile
    for index, value in enumerate((high_a, low_a, high_b, low_b)):
        again = jnp.where(line == index, value, again)
    tile = jnp.where(me[0] == SCAL // count, again, tile)
    if count > 8:
        tile = jnp.concatenate([tile, total[8:]], axis=0)
    tile = tile.astype(BF)
    for target in range(N_MANY):
        out[target] = tile


def middle(pieces, me):
    return pl.pallas_call(
        middle_kernel,
        out_shape=shape(*pieces.shape, dtype=BF),
        in_specs=[IN_VMEM, IN_SMEM],
        out_specs=IN_VMEM,
        compiler_params=PARAMS,
    )(pieces, me)


def final_kernel(arrived, tail, penalty, answer_out, residual_out):
    total = jnp.zeros((T, 640), F32)
    for source in range(N_ZH):
        total = total + arrived[source].astype(F32)
    square = total[:, 512:513] + total[:, 513:514]
    ridge = penalty[:, :1]
    mine = tail[:, :256]
    step = tail[:, 768:769] / (square + ridge * tail[:, 769:770])
    hess = total[:, :256] + total[:, 256:512] + ridge * mine
    answer_out[...] = tail[:, 256:512] + step * mine
    residual_out[...] = tail[:, 512:768] - step * hess


def shards(design, targets, factor, weights, penalty):
    zh = lax.axis_index("zh")
    me = lax.axis_index(MANY).reshape(1)
    low_factor = factor.astype(BF)
    slots = jnp.zeros((N_ZH, 256, RANK), BF)
    slots = lax.dynamic_update_slice(slots, low_factor[None], (zh, 0, 0))
    for shift in range(1, N_ZH):
        pairs = [(i, (i + shift) % N_ZH) for i in range(N_ZH)]
        other = lax.ppermute(low_factor, "zh", pairs)
        slots = lax.dynamic_update_slice(slots, other[None], ((zh - shift) % N_ZH, 0, 0))
    fac = slots.reshape(BLOCK, RANK)

    mat = exchange(pack(design, targets.T), OWN)
    arrived = exchange(call(start_kernel, shape(N_ZH, T, BLOCK + 256, dtype=BF))(mat), "zh")
    gram = lax.dot_general(fac, fac, (((0,), (0,)), ((), ())), preferred_element_type=F32)
    rest = call(cross_kernel, shape(2560, 128, dtype=BF))(mat, fac, gram)

    w = jnp.broadcast_to(weights[None, :], (8, RANK))
    ridge = jnp.broadcast_to(penalty[:, None], (T, 128))
    spot = zh.reshape(1)

    def over_many(packed):
        pieces = packed.reshape(N_MANY, -1, 128)
        total = middle(exchange(pieces, MANY), me)
        return exchange(total, MANY).reshape(packed.shape)

    packed, residual = first_call(arrived, mat, fac, rest)
    fix = residual
    answer = state = full = None
    for step_index in range(ITERS):
        first, last = step_index == 0, step_index == ITERS - 1
        back = over_many(packed)
        full = back if first else full
        send, state = search_call(
            first, last, back, spot, w, mat, residual, fac, state, full, answer, fix
        )
        arrived = exchange(send, "zh")
        if not last:
            packed, residual, answer = next_call(
                arrived, spot, ridge, mat, state, residual, fac, answer
            )
    answer, residual = call(final_kernel, (shape(T, 256), shape(T, 256)))(arrived, state, ridge)
    return answer.T, residual.T


def solution(mesh):
    finer = Mesh(mesh.devices.reshape(4, 2, 4, 4, 2), ("zh", "zl", "y", "x", "c"))
    spec = P((*FEAT, *ROW), None)
    in_specs = (P(ROW, FEAT), P(ROW, None), spec, P(), P())
    return jax.shard_map(
        shards, mesh=finer, in_specs=in_specs, out_specs=(spec, spec), check_vma=False
    )
```

time: 248 us -> 287 us (1.16)
  Pallas kernels: 12.1 us -> 83.7 us
  blocking collectives: 93.5 us -> 120 us
  local copies, waits for them, and re-layouts: 29.9 us -> 4.16 us
  waiting for transfers between devices: 55.3 us -> 39.1 us
  starting transfers between devices: 47.7 us -> 37.8 us
  other arithmetic: 6.49 us -> 0.03 us
    pallas_call x8 -> x12, Pallas kernels: 11.4 us -> 83 us  [the longest x1 66.1 us: pack(): pl.pallas_call(pack_kernel, out_shape=shape(8, 136, BLOCK, dtype=BF), in_...]
    all_to_all x6 -> x8, blocking collectives: 93.5 us -> 120 us  [exchange(): return lax.all_to_all(pieces, axes, 0, 0, tiled=True)]
    unnamed x82 -> x12, local copies, waits for them, and re-layouts: 22 us -> 1.58 us
    all_to_all x5 -> x3, waiting for transfers between devices: 53.5 us -> 37.2 us  [exchange(): return lax.all_to_all(pieces, axes, 0, 0, tiled=True)]
    all_to_all x5 -> x3, starting transfers between devices: 38.1 us -> 28.1 us  [exchange(): return lax.all_to_all(pieces, axes, 0, 0, tiled=True)]
    slice x12 -> x0, local copies, waits for them, and re-layouts: 5.19 us -> none  [the longest x6 2.32 us: split_again(): total = tile[0:4:2] + tile[1:4:2]]
  transfers between devices with their start and end apart: 8 -> 6, of which waited for: 6 -> 4; matrix products, arithmetic and copies ran while one was open for 2% -> 1% of each run, Pallas kernels for 1% -> 1%
where the time goes in v4:
time: 287 us; the launch traced here: 286 us
  blocking collectives  120 us (42%)
  Pallas kernels  83.7 us (29%)
  waiting for transfers between devices  39.1 us (14%)
  starting transfers between devices  37.8 us (13%)
  local copies, waits for them, and re-layouts  4.16 us (1%)
    all_to_all x8, blocking collectives, exchange(): return lax.all_to_all(pieces, axes, 0, 0, tiled=True)  120 us
    pallas_call x1, Pallas kernels, pack(): pl.pallas_call(pack_kernel, out_shape=shape(8, 136, BLOCK, dtype=BF), in_...  66.1 us
    all_to_all x3, waiting for transfers between devices, exchange(): return lax.all_to_all(pieces, axes, 0, 0, tiled=True)  37.2 us
    all_to_all x3, starting transfers between devices, exchange(): return lax.all_to_all(pieces, axes, 0, 0, tiled=True)  28.1 us
    ppermute x3, starting transfers between devices, shards(): other = lax.ppermute(low_factor, 'zh', pairs)  9.67 us
    pallas_call x3, Pallas kernels, search_call(): pl.pallas_call(lambda *refs: search_kernel(first, last, *refs), out_shape...  8.75 us
  transfers between devices with their start and end apart: 6, of which 4 were waited for; matrix products, arithmetic and copies ran while one was open for 1% of the time, Pallas kernels for 1%

profile of v4, /device:TPU:1, one launch (start us, length us, event | category | flops | bytes accessed | tf_op | source)
XLA Modules:
  0.0 285.8 jit_solution(9957521941049593611)
XLA Ops:
  0.6 66.1 %shard_map.68 = bf16[8,136,1024]{2,1,0:T(8,128)(2,1)} custom-call(bf16[128,8192]{1,0:T(8,128)(2,1)} %design.1, bf16[48,128]{1,0:T(8,128)(2,1)} %bitcast.37), custom_call_target="tpu_custom_call" | custom-call | tf_op jit(solution)/shard_map/pallas_call | solution.py:101
  66.7 0.0 copy-start.3
  66.7 6.5 %all-to-all-start = ((bf16[8,136,1024]{2,1,0:T(8,128)(2,1)}), bf16[8,136,1024]{2,1,0:T(8,128)(2,1)S(1)}, u32[]{:S(2)}, u32[]{:S(2)}) async-start(bf16[8,136,1024]{2,1,0:T(8,128)(2,1)} %shard_map.68), calls=%async_computation | async-start | bytes 4456448 | tf_op jit(solution)/shard_map/all_to_all | solution.py:23
  73.2 0.0 copy-done.3
  73.2 6.1 %collective-permute-start.1 = (bf16[256,256]{1,0:T(8,128)(2,1)S(1)}, bf16[256,256]{1,0:T(8,128)(2,1)}, u32[]{:S(2)}, u32[]{:S(2)}) collective-permute-start(bf16[256,256]{1,0:T(8,128)(2,1)S(1)} %convert_element_type.3), channel_id=1, source_target_pairs={{0,128},{64,192},{128,0},{192,64},{1,129},{65,193},{129,1},{193,65... | collective-permute-start | bytes 393224 | tf_op jit(solution)/shard_map/ppermute | solution.py:418
  79.3 1.2 collective-permute-start
  80.5 2.4 collective-permute-start.2
  82.9 18.6 %all-to-all-done.mat.refs_3_ = bf16[8,136,1024]{2,1,0:T(8,128)(2,1)S(1)} async-done(((bf16[8,136,1024]{2,1,0:T(8,128)(2,1)}), bf16[8,136,1024]{2,1,0:T(8,128)(2,1)S(1)}, u32[]{:S(2)}, u32[]{:S(2)}) %all-to-all-start) | async-done | bytes 2228256 | tf_op jit(solution)/shard_map/all_to_all | solution.py:23
  101.5 1.2 shard_map.69
  102.7 7.9 %all-to-all-start.1 = ((bf16[4,48,1280]{2,1,0:T(8,128)(2,1)}), bf16[4,48,1280]{2,1,0:T(8,128)(2,1)}, u32[]{:S(2)}, u32[]{:S(2)}) async-start(bf16[4,48,1280]{2,1,0:T(8,128)(2,1)} %shard_map.69), calls=%async_computation.1 | async-start | bytes 983040 | tf_op jit(solution)/shard_map/all_to_all | solution.py:23
  110.8 0.1 copy.7
  111.0 0.0 collective-permute-done.1
  111.0 1.0 copy.9
  112.0 1.8 collective-permute-done
  113.8 1.0 copy.8
  114.8 0.0 collective-permute-done.2
  114.9 0.1 copy.10
  115.0 0.2 copy.11
  115.2 0.3 convolution_bitcast_fusion.gram
  115.6 0.7 shard_map.70.rest
  116.3 3.9 %all-to-all-done.1.arrived = bf16[4,48,1280]{2,1,0:T(8,128)(2,1)} async-done(((bf16[4,48,1280]{2,1,0:T(8,128)(2,1)}), bf16[4,48,1280]{2,1,0:T(8,128)(2,1)}, u32[]{:S(2)}, u32[]{:S(2)}) %all-to-all-start.1) | async-done | bytes 491552 | tf_op jit(solution)/shard_map/all_to_all | solution.py:23
  120.2 2.3 shard_map.71
  122.5 0.0 copy-start
  122.5 0.7 copy-done
  123.2 0.9 copy-done.2
  124.1 13.7 %all-to-all-start.2 = ((bf16[64,48,128]{2,1,0:T(8,128)(2,1)}), bf16[64,48,128]{2,1,0:T(8,128)(2,1)S(1)}, u32[]{:S(2)}, u32[]{:S(2)}) async-start(bf16[64,48,128]{2,1,0:T(8,128)(2,1)} %bitcast.31), calls=%async_computation.2 | async-start | bytes 1572864 | tf_op jit(solution)/shard_map/all_to_all | solution.py:23
  137.8 14.7 %all-to-all-done.2.pieces = bf16[64,48,128]{2,1,0:T(8,128)(2,1)S(1)} async-done(((bf16[64,48,128]{2,1,0:T(8,128)(2,1)}), bf16[64,48,128]{2,1,0:T(8,128)(2,1)S(1)}, u32[]{:S(2)}, u32[]{:S(2)}) %all-to-all-start.2) | async-done | bytes 786464 | tf_op jit(solution)/shard_map/all_to_all | solution.py:23
  152.5 0.2 shard_map.72
  152.6 19.4 %all_to_all.55 = bf16[64,48,128]{2,1,0:T(8,128)(2,1)S(1)} all-to-all(bf16[64,48,128]{2,1,0:T(8,128)(2,1)S(1)} %shard_map.72), channel_id=1, replica_groups=mesh['zh'=4,'zl'=2,'y'=4,'x'=4,'c'=2] {'zl','y','x','c'}, dimensions={0} | all-to-all | bytes 1572864 | tf_op jit(solution)/shard_map/all_to_all | solution.py:23
  172.1 0.0 copy-done.4
  172.1 0.0 copy-done.1
  172.1 2.5 shard_map.73
  174.6 18.5 %all_to_all.56.refs_0_ = bf16[4,48,1152]{2,1,0:T(8,128)(2,1)S(1)} all-to-all(bf16[4,48,1152]{2,1,0:T(8,128)(2,1)S(1)} %get-tuple-element.20), channel_id=1, replica_groups=mesh['zh'=4,'zl'=2,'y'=4,'x'=4,'c'=2] {'zh'}, dimensions={0} | all-to-all | bytes 884736 | tf_op jit(solution)/shard_map/all_to_all | solution.py:23
  193.1 0.0 copy-done.5
  193.1 0.1 broadcast_in_dim.33.refs_2_.penalty
  193.2 1.6 shard_map.74
  194.8 14.6 %all_to_all.57.pieces = bf16[64,8,128]{2,1,0:T(8,128)(2,1)S(1)} all-to-all(bf16[64,8,128]{2,1,0:T(8,128)(2,1)S(1)} %bitcast.35), channel_id=1, replica_groups=mesh['zh'=4,'zl'=2,'y'=4,'x'=4,'c'=2] {'zl','y','x','c'}, dimensions={0} | all-to-all | bytes 262144 | tf_op jit(solution)/shard_map/all_to_all | solution.py:23
  209.4 0.1 shard_map.75
  209.5 12.6 %all_to_all.58 = bf16[64,8,128]{2,1,0:T(8,128)(2,1)S(1)} all-to-all(bf16[64,8,128]{2,1,0:T(8,128)(2,1)S(1)} %shard_map.75), channel_id=1, replica_groups=mesh['zh'=4,'zl'=2,'y'=4,'x'=4,'c'=2] {'zl','y','x','c'}, dimensions={0} | all-to-all | bytes 262144 | tf_op jit(solution)/shard_map/all_to_all | solution.py:23
  222.1 3.1 %shard_map.76 = (bf16[4,48,1152]{2,1,0:T(8,128)(2,1)S(1)}, f32[48,2432]{1,0:T(8,128)S(1)}) custom-call(bf16[512,128]{1,0:T(8,128)(2,1)S(1)} %bitcast.33, s32[1]{0:T(128)} %bitcast.10.refs_1_, f32[8,256]{1,0:T(8,128)S(1)} %broadcast_in_dim.32.refs_2_, bf16[8,136,1024]{2,1,0:T(8,128)(2,1)S(1)} %all-to-all-done.mat.refs_3_, ...), custom_call_target="tpu_custom_call" | custom-call | tf_op jit(solution)/shard_map/pallas_call | solution.py:354
  225.2 16.1 %all_to_all.59.refs_0_ = bf16[4,48,1152]{2,1,0:T(8,128)(2,1)S(1)} all-to-all(bf16[4,48,1152]{2,1,0:T(8,128)(2,1)S(1)} %get-tuple-element.24), channel_id=1, replica_groups=mesh['zh'=4,'zl'=2,'y'=4,'x'=4,'c'=2] {'zh'}, dimensions={0} | all-to-all | bytes 884736 | tf_op jit(solution)/shard_map/all_to_all | solution.py:23
  241.4 1.9 shard_map.77
  243.3 14.3 %all_to_all.60.pieces = bf16[64,8,128]{2,1,0:T(8,128)(2,1)S(1)} all-to-all(bf16[64,8,128]{2,1,0:T(8,128)(2,1)S(1)} %bitcast.34), channel_id=1, replica_groups=mesh['zh'=4,'zl'=2,'y'=4,'x'=4,'c'=2] {'zl','y','x','c'}, dimensions={0} | all-to-all | bytes 262144 | tf_op jit(solution)/shard_map/all_to_all | solution.py:23
  257.6 0.1 shard_map.78
  257.6 12.6 %all_to_all.61 = bf16[64,8,128]{2,1,0:T(8,128)(2,1)S(1)} all-to-all(bf16[64,8,128]{2,1,0:T(8,128)(2,1)S(1)} %shard_map.78), channel_id=1, replica_groups=mesh['zh'=4,'zl'=2,'y'=4,'x'=4,'c'=2] {'zl','y','x','c'}, dimensions={0} | all-to-all | bytes 262144 | tf_op jit(solution)/shard_map/all_to_all | solution.py:23
  270.3 3.2 %shard_map.79 = (bf16[4,48,640]{2,1,0:T(8,128)(2,1)S(1)}, f32[48,896]{1,0:T(8,128)S(1)}) custom-call(bf16[512,128]{1,0:T(8,128)(2,1)S(1)} %bitcast.32, s32[1]{0:T(128)} %bitcast.10.refs_1_, f32[8,256]{1,0:T(8,128)S(1)} %broadcast_in_dim.32.refs_2_, bf16[8,136,1024]{2,1,0:T(8,128)(2,1)S(1)} %all-to-all-done.mat.refs_3_, ...), custom_call_target="tpu_custom_call" | custom-call | tf_op jit(solution)/shard_map/pallas_call | solution.py:354
  273.5 11.6 %all_to_all.62.arrived = bf16[4,48,640]{2,1,0:T(8,128)(2,1)S(1)} all-to-all(bf16[4,48,640]{2,1,0:T(8,128)(2,1)S(1)} %get-tuple-element.30), channel_id=1, replica_groups=mesh['zh'=4,'zl'=2,'y'=4,'x'=4,'c'=2] {'zh'}, dimensions={0} | all-to-all | bytes 491520 | tf_op jit(solution)/shard_map/all_to_all | solution.py:23
  285.0 0.8 shard_map.80
  (12 shorter events, 0.1 us)
Async XLA Ops:
  66.7 6.5 %copy-start.3 = (f32[256,256]{1,0:T(8,128)S(1)}, f32[256,256]{1,0:T(8,128)}, u32[]{:S(2)}) copy-start(f32[256,256]{1,0:T(8,128)} %param.7) | copy-start | bytes 786436
  66.7 34.8 %all-to-all-start = ((bf16[8,136,1024]{2,1,0:T(8,128)(2,1)}), bf16[8,136,1024]{2,1,0:T(8,128)(2,1)S(1)}, u32[]{:S(2)}, u32[]{:S(2)}) async-start(bf16[8,136,1024]{2,1,0:T(8,128)(2,1)} %shard_map.68), calls=%async_computation | async-start | bytes 4456448 | tf_op jit(solution)/shard_map/all_to_all | solution.py:23
  73.2 37.7 %collective-permute-start.1 = (bf16[256,256]{1,0:T(8,128)(2,1)S(1)}, bf16[256,256]{1,0:T(8,128)(2,1)}, u32[]{:S(2)}, u32[]{:S(2)}) collective-permute-start(bf16[256,256]{1,0:T(8,128)(2,1)S(1)} %convert_element_type.3), channel_id=1, source_target_pairs={{0,128},{64,192},{128,0},{192,64},{1,129},{65,193},{129,1},{193,65... | collective-permute-start | bytes 393224 | tf_op jit(solution)/shard_map/ppermute | solution.py:418
  79.3 34.5 %collective-permute-start = (bf16[256,256]{1,0:T(8,128)(2,1)S(1)}, bf16[256,256]{1,0:T(8,128)(2,1)}, u32[]{:S(2)}, u32[]{:S(2)}) collective-permute-start(bf16[256,256]{1,0:T(8,128)(2,1)S(1)} %convert_element_type.3), channel_id=1, source_target_pairs={{0,64},{64,128},{128,192},{192,0},{1,65},{65,129},{129,193},{193,1... | collective-permute-start | bytes 393224 | tf_op jit(solution)/shard_map/ppermute | solution.py:418
  80.5 34.3 %collective-permute-start.2 = (bf16[256,256]{1,0:T(8,128)(2,1)S(1)}, bf16[256,256]{1,0:T(8,128)(2,1)S(1)}, u32[]{:S(2)}, u32[]{:S(2)}) collective-permute-start(bf16[256,256]{1,0:T(8,128)(2,1)S(1)} %convert_element_type.3), channel_id=1, source_target_pairs={{0,192},{64,0},{128,64},{192,128},{1,193},{65,1},{129,65},{193,129... | collective-permute-start | bytes 393224 | tf_op jit(solution)/shard_map/ppermute | solution.py:418
  102.7 17.5 %all-to-all-start.1 = ((bf16[4,48,1280]{2,1,0:T(8,128)(2,1)}), bf16[4,48,1280]{2,1,0:T(8,128)(2,1)}, u32[]{:S(2)}, u32[]{:S(2)}) async-start(bf16[4,48,1280]{2,1,0:T(8,128)(2,1)} %shard_map.69), calls=%async_computation.1 | async-start | bytes 983040 | tf_op jit(solution)/shard_map/all_to_all | solution.py:23
  122.5 0.7 copy-start
  123.2 0.9 copy-start.2
  124.1 48.0 %copy-start.4 = (f32[256]{0:T(256)S(1)}, f32[256]{0:T(256)}, u32[]{:S(2)}) copy-start(f32[256]{0:T(256)} %param.8) | copy-start | bytes 3076
  124.1 28.4 %all-to-all-start.2 = ((bf16[64,48,128]{2,1,0:T(8,128)(2,1)}), bf16[64,48,128]{2,1,0:T(8,128)(2,1)S(1)}, u32[]{:S(2)}, u32[]{:S(2)}) async-start(bf16[64,48,128]{2,1,0:T(8,128)(2,1)} %bitcast.31), calls=%async_computation.2 | async-start | bytes 1572864 | tf_op jit(solution)/shard_map/all_to_all | solution.py:23
  152.5 19.6 %copy-start.1 = (f32[48,1280]{1,0:T(8,128)S(1)}, f32[48,1280]{1,0:T(8,128)}, u32[]{:S(2)}) copy-start(f32[48,1280]{1,0:T(8,128)} %copy-done) | copy-start | bytes 737284
  172.1 21.0 %copy-start.5 = (f32[48]{0:T(128)S(1)}, f32[48]{0:T(128)}, u32[]{:S(2)}) copy-start(f32[48]{0:T(128)} %param.9) | copy-start | bytes 580

commit v5 on v4

--- a/solution.py
+++ b/solution.py
@@ -71,30 +71,39 @@
     return jnp.sum(array, axis=1, keepdims=True)
 
 
-def pack_kernel(design, goal, out, sems, goal_sems):
-    copies = []
+CHUNKS, DEEP = 4, 32
+
+
+def pack_kernel(design, goal, out, rows, packed, goals, sems):
+    def inward(index):
+        at = pl.ds(index * DEEP, DEEP)
+        return pltpu.make_async_copy(design.at[at, :], rows.at[at, :], sems.at[index])
+
+    def outward(index):
+        at = pl.ds(index * DEEP, DEEP)
+        return pltpu.make_async_copy(
+            packed.at[:, at, :], out.at[:, at, :], sems.at[CHUNKS + index]
+        )
+
+    for index in range(CHUNKS):
+        inward(index).start()
     for to in range(8):
-        for index in range(4):
-            at = (index * 8 + to) * 256
-            copies.append(
-                pltpu.make_async_copy(
-                    design.at[:, at : at + 256],
-                    out.at[to, :128, index * 256 : (index + 1) * 256],
-                    sems.at[to * 4 + index],
-                )
-            )
         for index in range(6):
-            copies.append(
-                pltpu.make_async_copy(
-                    goal.at[index * 8 : index * 8 + 8, :],
-                    out.at[to, 128:136, index * 128 : (index + 1) * 128],
-                    goal_sems.at[to * 6 + index],
-                )
-            )
-    for copy in copies:
-        copy.start()
-    for copy in copies:
-        copy.wait()
+            goals[to, :, index * 128 : (index + 1) * 128] = goal[index * 8 : index * 8 + 8, :]
+        goals[to, :, 768:] = jnp.zeros((8, 256), BF)
+    last = pltpu.make_async_copy(goals, out.at[:, 128:136, :], sems.at[2 * CHUNKS])
+    last.start()
+    for index in range(CHUNKS):
+        inward(index).wait()
+        low, high = index * DEEP, (index + 1) * DEEP
+        for to in range(8):
+            for part in range(4):
+                at = (part * 8 + to) * 256
+                packed[to, low:high, part * 256 : (part + 1) * 256] = rows[low:high, at : at + 256]
+        outward(index).start()
+    for index in range(CHUNKS):
+        outward(index).wait()
+    last.wait()
 
 
 def pack(design, goal):
@@ -103,7 +112,12 @@
         out_shape=shape(8, 136, BLOCK, dtype=BF),
         in_specs=[IN_HBM, IN_VMEM],
         out_specs=IN_HBM,
-        scratch_shapes=[pltpu.SemaphoreType.DMA((32,)), pltpu.SemaphoreType.DMA((48,))],
+        scratch_shapes=[
+            pltpu.VMEM((128, 8192), BF),
+            pltpu.VMEM((8, 128, BLOCK), BF),
+            pltpu.VMEM((8, 8, BLOCK), BF),
+            pltpu.SemaphoreType.DMA((2 * CHUNKS + 1,)),
+        ],
     )(design, goal)
 
 

time: 287 us -> 224 us (0.78)
  Pallas kernels: 83.7 us -> 20.9 us
    pallas_call x1, Pallas kernels: 66.1 us -> 3.24 us  [pack(): pl.pallas_call(pack_kernel, out_shape=shape(8, 136, BLOCK, dtype=BF), in_...]
where the time goes in v5:
time: 224 us; the launch traced here: 223 us
  blocking collectives  120 us (54%)
  waiting for transfers between devices  39.1 us (17%)
  starting transfers between devices  37.8 us (17%)
  Pallas kernels  20.9 us (9%)
  local copies, waits for them, and re-layouts  4.16 us (2%)
    all_to_all x8, blocking collectives, exchange(): return lax.all_to_all(pieces, axes, 0, 0, tiled=True)  120 us
    all_to_all x3, waiting for transfers between devices, exchange(): return lax.all_to_all(pieces, axes, 0, 0, tiled=True)  37.2 us
    all_to_all x3, starting transfers between devices, exchange(): return lax.all_to_all(pieces, axes, 0, 0, tiled=True)  28.1 us
    ppermute x3, starting transfers between devices, shards(): other = lax.ppermute(low_factor, 'zh', pairs)  9.67 us
    pallas_call x3, Pallas kernels, search_call(): pl.pallas_call(lambda *refs: search_kernel(first, last, *refs), out_shape...  8.75 us
  transfers between devices with their start and end apart: 6, of which 4 were waited for; matrix products, arithmetic and copies ran while one was open for 1% of the time, Pallas kernels for 1%

profile of v5, /device:TPU:1, one launch (start us, length us, event | category | flops | bytes accessed | tf_op | source)
XLA Modules:
  0.0 223.0 jit_solution(4059942892353156664)
XLA Ops:
  0.6 3.2 %shard_map.68 = bf16[8,136,1024]{2,1,0:T(8,128)(2,1)} custom-call(bf16[128,8192]{1,0:T(8,128)(2,1)} %design.1, bf16[48,128]{1,0:T(8,128)(2,1)} %bitcast.37), custom_call_target="tpu_custom_call" | custom-call | tf_op jit(solution)/shard_map/pallas_call | solution.py:110
  3.9 0.0 copy-start.3
  3.9 6.5 %all-to-all-start = ((bf16[8,136,1024]{2,1,0:T(8,128)(2,1)}), bf16[8,136,1024]{2,1,0:T(8,128)(2,1)S(1)}, u32[]{:S(2)}, u32[]{:S(2)}) async-start(bf16[8,136,1024]{2,1,0:T(8,128)(2,1)} %shard_map.68), calls=%async_computation | async-start | bytes 4456448 | tf_op jit(solution)/shard_map/all_to_all | solution.py:23
  10.4 0.0 copy-done.3
  10.4 6.1 %collective-permute-start.1 = (bf16[256,256]{1,0:T(8,128)(2,1)S(1)}, bf16[256,256]{1,0:T(8,128)(2,1)}, u32[]{:S(2)}, u32[]{:S(2)}) collective-permute-start(bf16[256,256]{1,0:T(8,128)(2,1)S(1)} %convert_element_type.3), channel_id=1, source_target_pairs={{0,128},{64,192},{128,0},{192,64},{1,129},{65,193},{129,1},{193,65... | collective-permute-start | bytes 393224 | tf_op jit(solution)/shard_map/ppermute | solution.py:432
  16.5 1.2 collective-permute-start
  17.7 2.4 %collective-permute-start.2 = (bf16[256,256]{1,0:T(8,128)(2,1)S(1)}, bf16[256,256]{1,0:T(8,128)(2,1)S(1)}, u32[]{:S(2)}, u32[]{:S(2)}) collective-permute-start(bf16[256,256]{1,0:T(8,128)(2,1)S(1)} %convert_element_type.3), channel_id=1, source_target_pairs={{0,192},{64,0},{128,64},{192,128},{1,193},{65,1},{129,65},{193,129... | collective-permute-start | bytes 393224 | tf_op jit(solution)/shard_map/ppermute | solution.py:432
  20.1 18.6 %all-to-all-done.mat.refs_3_ = bf16[8,136,1024]{2,1,0:T(8,128)(2,1)S(1)} async-done(((bf16[8,136,1024]{2,1,0:T(8,128)(2,1)}), bf16[8,136,1024]{2,1,0:T(8,128)(2,1)S(1)}, u32[]{:S(2)}, u32[]{:S(2)}) %all-to-all-start) | async-done | bytes 2228256 | tf_op jit(solution)/shard_map/all_to_all | solution.py:23
  38.7 1.2 shard_map.69
  39.9 7.9 %all-to-all-start.1 = ((bf16[4,48,1280]{2,1,0:T(8,128)(2,1)}), bf16[4,48,1280]{2,1,0:T(8,128)(2,1)}, u32[]{:S(2)}, u32[]{:S(2)}) async-start(bf16[4,48,1280]{2,1,0:T(8,128)(2,1)} %shard_map.69), calls=%async_computation.1 | async-start | bytes 983040 | tf_op jit(solution)/shard_map/all_to_all | solution.py:23
  48.0 0.1 copy.7
  48.2 0.0 collective-permute-done.1
  48.2 1.0 copy.9
  49.2 1.8 collective-permute-done
  51.0 1.0 copy.8
  52.0 0.0 collective-permute-done.2
  52.0 0.1 copy.10
  52.2 0.2 copy.11
  52.4 0.3 convolution_bitcast_fusion.gram
  52.8 0.7 shard_map.70.rest
  53.5 3.9 %all-to-all-done.1.arrived = bf16[4,48,1280]{2,1,0:T(8,128)(2,1)} async-done(((bf16[4,48,1280]{2,1,0:T(8,128)(2,1)}), bf16[4,48,1280]{2,1,0:T(8,128)(2,1)}, u32[]{:S(2)}, u32[]{:S(2)}) %all-to-all-start.1) | async-done | bytes 491552 | tf_op jit(solution)/shard_map/all_to_all | solution.py:23
  57.4 2.3 %shard_map.71 = (bf16[3072,128]{1,0:T(8,128)(2,1)S(1)}, f32[48,1280]{1,0:T(8,128)S(1)}) custom-call(bf16[4,48,1280]{2,1,0:T(8,128)(2,1)} %all-to-all-done.1.arrived, bf16[8,136,1024]{2,1,0:T(8,128)(2,1)S(1)} %all-to-all-done.mat.refs_3_, bf16[1024,256]{1,0:T(8,128)(2,1)S(1)} %bitcast.22, bf16[2560,128]{1,0:T(8,128)(2,1)S(1)} %shard_map.70.rest), custom_call_target="tpu_custom_call" | custom-call | tf_op jit(solution)/shard_map/pallas_call | solution.py:177
  59.7 0.0 copy-start
  59.7 0.7 copy-done
  60.4 0.9 copy-done.2
  61.3 13.7 %all-to-all-start.2 = ((bf16[64,48,128]{2,1,0:T(8,128)(2,1)}), bf16[64,48,128]{2,1,0:T(8,128)(2,1)S(1)}, u32[]{:S(2)}, u32[]{:S(2)}) async-start(bf16[64,48,128]{2,1,0:T(8,128)(2,1)} %bitcast.31), calls=%async_computation.2 | async-start | bytes 1572864 | tf_op jit(solution)/shard_map/all_to_all | solution.py:23
  74.9 14.7 %all-to-all-done.2.pieces = bf16[64,48,128]{2,1,0:T(8,128)(2,1)S(1)} async-done(((bf16[64,48,128]{2,1,0:T(8,128)(2,1)}), bf16[64,48,128]{2,1,0:T(8,128)(2,1)S(1)}, u32[]{:S(2)}, u32[]{:S(2)}) %all-to-all-start.2) | async-done | bytes 786464 | tf_op jit(solution)/shard_map/all_to_all | solution.py:23
  89.7 0.2 shard_map.72
  89.8 19.4 %all_to_all.55 = bf16[64,48,128]{2,1,0:T(8,128)(2,1)S(1)} all-to-all(bf16[64,48,128]{2,1,0:T(8,128)(2,1)S(1)} %shard_map.72), channel_id=1, replica_groups=mesh['zh'=4,'zl'=2,'y'=4,'x'=4,'c'=2] {'zl','y','x','c'}, dimensions={0} | all-to-all | bytes 1572864 | tf_op jit(solution)/shard_map/all_to_all | solution.py:23
  109.2 0.0 copy-done.4
  109.3 0.0 copy-done.1
  109.3 2.5 %shard_map.73 = (bf16[4,48,1152]{2,1,0:T(8,128)(2,1)S(1)}, f32[48,2432]{1,0:T(8,128)S(1)}) custom-call(bf16[3072,128]{1,0:T(8,128)(2,1)S(1)} %bitcast.28, s32[1]{0:T(128)} %bitcast.10.refs_1_, f32[8,256]{1,0:T(8,128)S(1)} %broadcast_in_dim.32.refs_2_, bf16[8,136,1024]{2,1,0:T(8,128)(2,1)S(1)} %all-to-all-done.mat.refs_3_, f32[48,1280]{1,0:T(8,128)S(1)} %copy-done.1, ...), custom_call_target="tpu_custom_call" | custom-call | tf_op jit(solution)/shard_map/pallas_call | solution.py:368
  111.7 18.5 %all_to_all.56.refs_0_ = bf16[4,48,1152]{2,1,0:T(8,128)(2,1)S(1)} all-to-all(bf16[4,48,1152]{2,1,0:T(8,128)(2,1)S(1)} %get-tuple-element.20), channel_id=1, replica_groups=mesh['zh'=4,'zl'=2,'y'=4,'x'=4,'c'=2] {'zh'}, dimensions={0} | all-to-all | bytes 884736 | tf_op jit(solution)/shard_map/all_to_all | solution.py:23
  130.3 0.0 copy-done.5
  130.3 0.1 broadcast_in_dim.33.refs_2_.penalty
  130.3 1.6 shard_map.74
  132.0 14.6 %all_to_all.57.pieces = bf16[64,8,128]{2,1,0:T(8,128)(2,1)S(1)} all-to-all(bf16[64,8,128]{2,1,0:T(8,128)(2,1)S(1)} %bitcast.35), channel_id=1, replica_groups=mesh['zh'=4,'zl'=2,'y'=4,'x'=4,'c'=2] {'zl','y','x','c'}, dimensions={0} | all-to-all | bytes 262144 | tf_op jit(solution)/shard_map/all_to_all | solution.py:23
  146.6 0.1 shard_map.75
  146.7 12.6 %all_to_all.58 = bf16[64,8,128]{2,1,0:T(8,128)(2,1)S(1)} all-to-all(bf16[64,8,128]{2,1,0:T(8,128)(2,1)S(1)} %shard_map.75), channel_id=1, replica_groups=mesh['zh'=4,'zl'=2,'y'=4,'x'=4,'c'=2] {'zl','y','x','c'}, dimensions={0} | all-to-all | bytes 262144 | tf_op jit(solution)/shard_map/all_to_all | solution.py:23
  159.3 3.1 %shard_map.76 = (bf16[4,48,1152]{2,1,0:T(8,128)(2,1)S(1)}, f32[48,2432]{1,0:T(8,128)S(1)}) custom-call(bf16[512,128]{1,0:T(8,128)(2,1)S(1)} %bitcast.33, s32[1]{0:T(128)} %bitcast.10.refs_1_, f32[8,256]{1,0:T(8,128)S(1)} %broadcast_in_dim.32.refs_2_, bf16[8,136,1024]{2,1,0:T(8,128)(2,1)S(1)} %all-to-all-done.mat.refs_3_, ...), custom_call_target="tpu_custom_call" | custom-call | tf_op jit(solution)/shard_map/pallas_call | solution.py:368
  162.4 16.1 %all_to_all.59.refs_0_ = bf16[4,48,1152]{2,1,0:T(8,128)(2,1)S(1)} all-to-all(bf16[4,48,1152]{2,1,0:T(8,128)(2,1)S(1)} %get-tuple-element.24), channel_id=1, replica_groups=mesh['zh'=4,'zl'=2,'y'=4,'x'=4,'c'=2] {'zh'}, dimensions={0} | all-to-all | bytes 884736 | tf_op jit(solution)/shard_map/all_to_all | solution.py:23
  178.6 1.9 shard_map.77
  180.5 14.3 %all_to_all.60.pieces = bf16[64,8,128]{2,1,0:T(8,128)(2,1)S(1)} all-to-all(bf16[64,8,128]{2,1,0:T(8,128)(2,1)S(1)} %bitcast.34), channel_id=1, replica_groups=mesh['zh'=4,'zl'=2,'y'=4,'x'=4,'c'=2] {'zl','y','x','c'}, dimensions={0} | all-to-all | bytes 262144 | tf_op jit(solution)/shard_map/all_to_all | solution.py:23
  194.7 0.1 shard_map.78
  194.8 12.6 %all_to_all.61 = bf16[64,8,128]{2,1,0:T(8,128)(2,1)S(1)} all-to-all(bf16[64,8,128]{2,1,0:T(8,128)(2,1)S(1)} %shard_map.78), channel_id=1, replica_groups=mesh['zh'=4,'zl'=2,'y'=4,'x'=4,'c'=2] {'zl','y','x','c'}, dimensions={0} | all-to-all | bytes 262144 | tf_op jit(solution)/shard_map/all_to_all | solution.py:23
  207.5 3.2 %shard_map.79 = (bf16[4,48,640]{2,1,0:T(8,128)(2,1)S(1)}, f32[48,896]{1,0:T(8,128)S(1)}) custom-call(bf16[512,128]{1,0:T(8,128)(2,1)S(1)} %bitcast.32, s32[1]{0:T(128)} %bitcast.10.refs_1_, f32[8,256]{1,0:T(8,128)S(1)} %broadcast_in_dim.32.refs_2_, bf16[8,136,1024]{2,1,0:T(8,128)(2,1)S(1)} %all-to-all-done.mat.refs_3_, ...), custom_call_target="tpu_custom_call" | custom-call | tf_op jit(solution)/shard_map/pallas_call | solution.py:368
  210.6 11.6 %all_to_all.62.arrived = bf16[4,48,640]{2,1,0:T(8,128)(2,1)S(1)} all-to-all(bf16[4,48,640]{2,1,0:T(8,128)(2,1)S(1)} %get-tuple-element.30), channel_id=1, replica_groups=mesh['zh'=4,'zl'=2,'y'=4,'x'=4,'c'=2] {'zh'}, dimensions={0} | all-to-all | bytes 491520 | tf_op jit(solution)/shard_map/all_to_all | solution.py:23
  222.2 0.8 shard_map.80
  (12 shorter events, 0.1 us)
Async XLA Ops:
  3.9 6.5 %copy-start.3 = (f32[256,256]{1,0:T(8,128)S(1)}, f32[256,256]{1,0:T(8,128)}, u32[]{:S(2)}) copy-start(f32[256,256]{1,0:T(8,128)} %param.7) | copy-start | bytes 786436
  3.9 34.8 %all-to-all-start = ((bf16[8,136,1024]{2,1,0:T(8,128)(2,1)}), bf16[8,136,1024]{2,1,0:T(8,128)(2,1)S(1)}, u32[]{:S(2)}, u32[]{:S(2)}) async-start(bf16[8,136,1024]{2,1,0:T(8,128)(2,1)} %shard_map.68), calls=%async_computation | async-start | bytes 4456448 | tf_op jit(solution)/shard_map/all_to_all | solution.py:23
  10.4 37.7 %collective-permute-start.1 = (bf16[256,256]{1,0:T(8,128)(2,1)S(1)}, bf16[256,256]{1,0:T(8,128)(2,1)}, u32[]{:S(2)}, u32[]{:S(2)}) collective-permute-start(bf16[256,256]{1,0:T(8,128)(2,1)S(1)} %convert_element_type.3), channel_id=1, source_target_pairs={{0,128},{64,192},{128,0},{192,64},{1,129},{65,193},{129,1},{193,65... | collective-permute-start | bytes 393224 | tf_op jit(solution)/shard_map/ppermute | solution.py:432
  16.5 34.5 %collective-permute-start = (bf16[256,256]{1,0:T(8,128)(2,1)S(1)}, bf16[256,256]{1,0:T(8,128)(2,1)}, u32[]{:S(2)}, u32[]{:S(2)}) collective-permute-start(bf16[256,256]{1,0:T(8,128)(2,1)S(1)} %convert_element_type.3), channel_id=1, source_target_pairs={{0,64},{64,128},{128,192},{192,0},{1,65},{65,129},{129,193},{193,1... | collective-permute-start | bytes 393224 | tf_op jit(solution)/shard_map/ppermute | solution.py:432
  17.7 34.3 %collective-permute-start.2 = (bf16[256,256]{1,0:T(8,128)(2,1)S(1)}, bf16[256,256]{1,0:T(8,128)(2,1)S(1)}, u32[]{:S(2)}, u32[]{:S(2)}) collective-permute-start(bf16[256,256]{1,0:T(8,128)(2,1)S(1)} %convert_element_type.3), channel_id=1, source_target_pairs={{0,192},{64,0},{128,64},{192,128},{1,193},{65,1},{129,65},{193,129... | collective-permute-start | bytes 393224 | tf_op jit(solution)/shard_map/ppermute | solution.py:432
  39.9 17.5 %all-to-all-start.1 = ((bf16[4,48,1280]{2,1,0:T(8,128)(2,1)}), bf16[4,48,1280]{2,1,0:T(8,128)(2,1)}, u32[]{:S(2)}, u32[]{:S(2)}) async-start(bf16[4,48,1280]{2,1,0:T(8,128)(2,1)} %shard_map.69), calls=%async_computation.1 | async-start | bytes 983040 | tf_op jit(solution)/shard_map/all_to_all | solution.py:23
  59.7 0.7 copy-start
  60.4 0.9 copy-start.2
  61.3 48.0 %copy-start.4 = (f32[256]{0:T(256)S(1)}, f32[256]{0:T(256)}, u32[]{:S(2)}) copy-start(f32[256]{0:T(256)} %param.8) | copy-start | bytes 3076
  61.3 28.4 %all-to-all-start.2 = ((bf16[64,48,128]{2,1,0:T(8,128)(2,1)}), bf16[64,48,128]{2,1,0:T(8,128)(2,1)S(1)}, u32[]{:S(2)}, u32[]{:S(2)}) async-start(bf16[64,48,128]{2,1,0:T(8,128)(2,1)} %bitcast.31), calls=%async_computation.2 | async-start | bytes 1572864 | tf_op jit(solution)/shard_map/all_to_all | solution.py:23
  89.7 19.6 %copy-start.1 = (f32[48,1280]{1,0:T(8,128)S(1)}, f32[48,1280]{1,0:T(8,128)}, u32[]{:S(2)}) copy-start(f32[48,1280]{1,0:T(8,128)} %copy-done) | copy-start | bytes 737284
  109.3 21.0 %copy-start.5 = (f32[48]{0:T(128)S(1)}, f32[48]{0:T(128)}, u32[]{:S(2)}) copy-start(f32[48]{0:T(128)} %param.9) | copy-start | bytes 580
